TPU v7x, 32 devices: a whole 2x2x4 slice. The times are simulated.
32 devices in a mesh: seq: 16 (over z, y, core), head: 2 (over x).
Axes of the slice: x: 2, y: 2, z: 4, core: 2. Of those that a mesh axis runs over, the one named last changes fastest.
Arguments:
- tokens: bfloat16 [8192, 1024], P('seq'), may hold values from -24 to 24
- norm_attn: float32 [1024], replicated, may hold values from 0.5 to 1.5
- self_qkv: bfloat16 [3, 1024, 1024], P(None, None, 'head'), may hold values from -4 to 4
- self_out: bfloat16 [1024, 1024], P('head'), may hold values from -0.1875 to 0.1875
- norm_ffn: float32 [1024], replicated, may hold values from 0.5 to 1.5
- ffn_in: bfloat16 [2, 1024, 2816], P(None, None, 'head'), may hold values from -0.1875 to 0.1875
- ffn_out: bfloat16 [2816, 1024], P('head'), may hold values from -0.109375 to 0.109375
- norm_final: float32 [1024], replicated, may hold values from 0.5 to 1.5
- pad_lengths: int32 [16], replicated, may hold values from 64 to 512
- targets: bfloat16 [512, 1024], replicated, may hold values from -8 to 8
- target_lengths: int32 [4], replicated, may hold values from 32 to 128
- norm_cross: float32 [1024], replicated, may hold values from 0.1 to 1.9
- cross_query: bfloat16 [1024, 1024], P(None, 'head'), may hold values from -4 to 4
- cross_kv: bfloat16 [2, 1024, 1024], P(None, None, 'head'), may hold values from -4 to 4
- cross_out: bfloat16 [1024, 1024], P('head'), may hold values from -4 to 4
Outputs:
- encoded: bfloat16 [8192, 1024], P('seq')
- decoded: bfloat16 [512, 1024], replicated
All inputs are finite; a program needn't handle non-finite values.
Results may differ from a plain program's by a relative error of at most 0.033.
Values may be sent and summed in bfloat16 or wider, within the bound.
A program may use at most 128 MiB of HBM per device.

v0:
```python
import math

import jax
import jax.numpy as jnp
from jax import lax
from jax.sharding import PartitionSpec as P

HD = 64
TOK_DEV = 512
TGT_LEN = 128


epsilon = 1e-06
masked_score = -1e30


def rms_norm(values, gain_vector):
    widened = values.astype(jnp.float32)
    return (
        widened
        * lax.rsqrt(jnp.mean(widened * widened, axis=-1, keepdims=True) + epsilon)
        * gain_vector
    )


def spread_heads(per_head):
    return jnp.repeat(per_head.T, HD, axis=1)


def live_within(positions, lengths, span):
    block_ids = jnp.arange(lengths.shape[0], dtype=jnp.int32)
    owners = positions // span
    lengths_here = jnp.sum(
        jnp.where(owners[:, None] == block_ids[None, :], lengths[None, :], 0), axis=1
    )
    return positions % span < lengths_here


def live_keys(positions, pad_lengths):
    return live_within(positions, pad_lengths, TOK_DEV)


def flash_block(flash_state, query_heads, key_rows, value_rows, live_rows, scaling):
    running_max, running_sum, running_acc = flash_state
    key_count = key_rows.shape[0]
    heads_here = query_heads.shape[1]
    keys_split = key_rows.reshape(key_count, heads_here, HD)
    values_split = value_rows.reshape(key_count, heads_here, HD)
    scores = (
        jnp.einsum("qhd,khd->hqk", query_heads, keys_split, preferred_element_type=jnp.float32)
        * scaling
    )
    scores = jnp.where(live_rows[None, None, :], scores, masked_score)
    new_max = jnp.maximum(running_max, jnp.max(scores, axis=-1))
    shrink = jnp.exp(running_max - new_max)
    weights = jnp.where(live_rows[None, None, :], jnp.exp(scores - new_max[:, :, None]), 0.0)
    new_sum = running_sum * shrink + jnp.sum(weights, axis=-1)
    mixed_values = jnp.einsum(
        "hqk,khd->qhd",
        weights.astype(jnp.bfloat16),
        values_split,
        preferred_element_type=jnp.float32,
    )
    new_acc = running_acc * spread_heads(shrink) + mixed_values.reshape(
        mixed_values.shape[0], heads_here * HD
    )
    return (new_max, new_sum, new_acc)


def feed_forward(normed_in, ffn_in, ffn_out):
    gate_proj = jnp.dot(normed_in, ffn_in[0], preferred_element_type=jnp.float32)
    up_proj = jnp.dot(normed_in, ffn_in[1], preferred_element_type=jnp.float32)
    activated = (jax.nn.gelu(gate_proj, approximate=True) * up_proj).astype(jnp.bfloat16)
    return jnp.dot(activated, ffn_out, preferred_element_type=jnp.float32)


def local(
    tokens,
    norm_attn,
    self_qkv,
    self_out,
    norm_ffn,
    ffn_in,
    ffn_out,
    norm_final,
    pad_lengths,
    targets,
    target_lengths,
    norm_cross,
    cross_query,
    cross_kv,
    cross_out,
):
    row_count = tokens.shape[0]
    heads_here = self_qkv.shape[2] // HD
    scaling = HD ** (-0.5)
    normed = rms_norm(tokens, norm_attn).astype(jnp.bfloat16)
    queries = jnp.dot(normed, self_qkv[0], preferred_element_type=jnp.float32).astype(jnp.bfloat16)
    keys_local = jnp.dot(normed, self_qkv[1], preferred_element_type=jnp.float32).astype(
        jnp.bfloat16
    )
    values_local = jnp.dot(normed, self_qkv[2], preferred_element_type=jnp.float32).astype(
        jnp.bfloat16
    )
    query_heads = queries.reshape(row_count, heads_here, HD)
    start_state = (
        jnp.full((heads_here, row_count), masked_score, jnp.float32),
        jnp.zeros((heads_here, row_count), jnp.float32),
        jnp.zeros((row_count, heads_here * HD), jnp.float32),
    )
    key_piece = lax.all_gather(keys_local, "seq", axis=0, tiled=True)
    value_piece = lax.all_gather(values_local, "seq", axis=0, tiled=True)
    piece_rows = key_piece.shape[0]
    block_width = math.gcd(piece_rows, 2048)

    def step_once(inner_state, block_index):
        first_row = block_index * block_width
        key_rows = lax.dynamic_slice_in_dim(key_piece, first_row, block_width, 0)
        value_rows = lax.dynamic_slice_in_dim(value_piece, first_row, block_width, 0)
        positions = first_row + jnp.arange(block_width, dtype=jnp.int32)
        updated = flash_block(
            inner_state,
            query_heads,
            key_rows,
            value_rows,
            live_keys(positions, pad_lengths),
            scaling,
        )
        return (updated, None)

    final_state, unused = lax.scan(
        step_once, start_state, jnp.arange(piece_rows // block_width, dtype=jnp.int32)
    )
    final_max, final_sum, final_acc = final_state
    context = (final_acc / spread_heads(final_sum)).astype(jnp.bfloat16)
    attn_part = jnp.dot(context, self_out, preferred_element_type=jnp.float32)
    hidden_in = tokens.astype(jnp.float32) + lax.psum(
        attn_part.astype(jnp.bfloat16), "head"
    ).astype(jnp.float32)
    ffn_normed = rms_norm(hidden_in, norm_ffn).astype(jnp.bfloat16)
    ffn_part = feed_forward(ffn_normed, ffn_in, ffn_out)
    final_in = hidden_in + lax.psum(ffn_part.astype(jnp.bfloat16), "head").astype(jnp.float32)
    encoded = rms_norm(final_in, norm_final).astype(jnp.bfloat16)
    target_rows = targets.shape[0]
    cross_normed = rms_norm(targets, norm_cross).astype(jnp.bfloat16)
    cross_queries = jnp.dot(cross_normed, cross_query, preferred_element_type=jnp.float32).astype(
        jnp.bfloat16
    )
    cross_keys = jnp.dot(encoded, cross_kv[0], preferred_element_type=jnp.float32).astype(
        jnp.bfloat16
    )
    cross_values = jnp.dot(encoded, cross_kv[1], preferred_element_type=jnp.float32).astype(
        jnp.bfloat16
    )
    cross_heads = cross_queries.reshape(target_rows, heads_here, HD)
    keys_split = cross_keys.reshape(row_count, heads_here, HD)
    values_split = cross_values.reshape(row_count, heads_here, HD)
    positions = lax.axis_index("seq") * row_count + jnp.arange(row_count, dtype=jnp.int32)
    live_here = live_keys(positions, pad_lengths)
    cross_scores = (
        jnp.einsum("qhd,khd->hqk", cross_heads, keys_split, preferred_element_type=jnp.float32)
        * scaling
    )
    cross_scores = jnp.where(live_here[None, None, :], cross_scores, masked_score)
    local_max = jnp.max(cross_scores, axis=-1)
    global_max = lax.pmax(local_max, "seq")
    weights = jnp.where(
        live_here[None, None, :], jnp.exp(cross_scores - global_max[:, :, None]), 0.0
    )
    local_sum = jnp.sum(weights, axis=-1)
    local_mixed = jnp.einsum(
        "hqk,khd->qhd",
        weights.astype(jnp.bfloat16),
        values_split,
        preferred_element_type=jnp.float32,
    )
    weight_sum, mixed_values = (
        lax.psum(local_sum.astype(jnp.bfloat16), "seq").astype(jnp.float32),
        lax.psum(
            local_mixed.reshape(target_rows, heads_here * HD).astype(jnp.bfloat16), "seq"
        ).astype(jnp.float32),
    )
    cross_context = (mixed_values / spread_heads(weight_sum)).astype(jnp.bfloat16)
    cross_part = jnp.dot(cross_context, cross_out, preferred_element_type=jnp.float32)
    cross_total = lax.psum(cross_part.astype(jnp.bfloat16), "head").astype(jnp.float32)
    slots = jnp.arange(target_rows, dtype=jnp.int32)
    target_live = slots % TGT_LEN < jnp.repeat(
        target_lengths, TGT_LEN, total_repeat_length=target_rows
    )
    decoded = (
        targets.astype(jnp.float32) + jnp.where(target_live[:, None], cross_total, 0.0)
    ).astype(jnp.bfloat16)
    return (encoded, decoded)


def solution(mesh):
    placed = (
        P("seq", None),
        P(),
        P(None, None, "head"),
        P("head", None),
        P(),
        P(None, None, "head"),
        P("head", None),
        P(),
        P(),
        P(),
        P(),
        P(),
        P(None, "head"),
        P(None, None, "head"),
        P("head", None),
    )
    return jax.shard_map(
        local, mesh=mesh, in_specs=placed, out_specs=(P("seq", None), P()), check_vma=False
    )
```

profile of v0, /device:TPU:0, one launch (start us, length us, event | category | flops | bytes accessed | tf_op | source)
XLA Modules:
  0.0 726.6 jit_solution(55890220503606311)
XLA Ops:
  7.2 1.7 fusion.38
  8.9 3.1 convolution_convert_fusion.8
  12.1 3.1 convolution_convert_fusion.6
  15.3 2.4 convolution_convert_fusion.7
  17.7 71.5 %all-gather.3.cloned.1.call-done = bf16[8192,512]{1,0:T(8,128)(2,1)} async-done(((bf16[512,512]{1,0:T(8,128)(2,1)}), bf16[8192,512]{1,0:T(8,128)(2,1)}) %all-gather.3.cloned.1.call-update) | async-done | bytes 8388624 | tf_op jit(solution)/shard_map/all_gather | solution.py:111
  89.2 75.1 %all-gather.5.cloned.1.call-done = bf16[8192,512]{1,0:T(8,128)(2,1)} async-done(((bf16[512,512]{1,0:T(8,128)(2,1)}), bf16[8192,512]{1,0:T(8,128)(2,1)}) %all-gather.5.cloned.1.call-update) | async-done | bytes 8388624 | tf_op jit(solution)/shard_map/all_gather | solution.py:112
  164.3 242.0 %while.18 = (s32[]{:T(128)}, f32[8,512]{1,0:T(8,128)S(1)}, f32[8,512]{1,0:T(8,128)S(1)}, f32[512,512]{0,1:T(8,128)}, s32[4]{0:T(128)S(1)}, /*index=5*/s32[16]{0:...) while((s32[]{:T(128)}, f32[8,512]{1,0:T(8,128)S(1)}, ...), condition=%wide.region_5.6_spmd.clone, body=%wide.region_1.5_spmd.clone.sunk | while | flops 2257502208 | bytes 135045456 | solution.py:131
  164.3 0.6 dynamic_slice.27
  165.5 4.5 constant_dynamic-slice_fusion.3
  170.0 4.0 copy.31
  174.1 15.6 %bitcast_reduce_fusion.2 = (f32[8,512]{1,0:T(8,128)S(1)}, f32[8,2048,512]{2,1,0:T(8,128)}) fusion(pred[2048]{0:T(1024)(128)(4,1)S(1)} %fusion.113, bf16[2048,8,64]{0,2,1:T(8,128)(2,1)} %bitcast.120, bf16[512,8,64]{0,2,1:T(8,128)(2,1)S(1)} %get-tuple-element.311), kind=kOutput, calls=%fused_computation.1.clone.1 | convolution fusion | flops 1098903552 | bytes 36194304 | tf_op jit(solution)/shard_map/while/body/eval_jaxpr/qhd,khd->hqk/dot_general | solution.py:50
  189.7 4.0 copy.32
  193.7 14.9 %fusion.117 = f32[8,64,512]{2,1,0:T(8,128)S(1)} fusion(bf16[2048,8,64]{0,2,1:T(8,128)(2,1)} %bitcast.121, f32[8,2048,512]{2,1,0:T(8,128)} %get-tuple-element.275, f32[8,512]{1,0:T(8,128)S(1)} %get-tuple-element.305, pred[2048]{0:T(1024)(128)(4,1)S(1)} %fusion.113), kind=kOutput, calls=%fused_computation.7.clone.1 | convolution fusion | flops 1115684864 | bytes 36718592 | tf_op jit(solution)/shard_map/while/body/eval_jaxpr/hqk,khd->qhd/dot_general | solution.py:58
  208.7 0.3 bitcast_add_fusion.2
  209.0 15.7 %fusion.115 = f32[8,512]{1,0:T(8,128)S(1)} fusion(f32[8,2048,512]{2,1,0:T(8,128)} %get-tuple-element.275, f32[8,512]{1,0:T(8,128)S(1)} %get-tuple-element.305, pred[2048]{0:T(1024)(128)(4,1)S(1)} %fusion.113), kind=kLoop, calls=%fused_computation.6.clone.1 | loop fusion | flops 41938944 | bytes 33589248 | tf_op jit(solution)/shard_map/while/body/eval_jaxpr/reduce_sum | solution.py:57
  224.8 0.6 dynamic_slice.27
  226.0 4.5 constant_dynamic-slice_fusion.3
  230.5 4.0 copy.31
  234.6 15.6 %bitcast_reduce_fusion.2 = (f32[8,512]{1,0:T(8,128)S(1)}, f32[8,2048,512]{2,1,0:T(8,128)}) fusion(pred[2048]{0:T(1024)(128)(4,1)S(1)} %fusion.113, bf16[2048,8,64]{0,2,1:T(8,128)(2,1)} %bitcast.120, bf16[512,8,64]{0,2,1:T(8,128)(2,1)S(1)} %get-tuple-element.311), kind=kOutput, calls=%fused_computation.1.clone.1 | convolution fusion | flops 1098903552 | bytes 36194304 | tf_op jit(solution)/shard_map/while/body/eval_jaxpr/qhd,khd->hqk/dot_general | solution.py:50
  250.3 4.0 copy.32
  254.2 14.9 %fusion.117 = f32[8,64,512]{2,1,0:T(8,128)S(1)} fusion(bf16[2048,8,64]{0,2,1:T(8,128)(2,1)} %bitcast.121, f32[8,2048,512]{2,1,0:T(8,128)} %get-tuple-element.275, f32[8,512]{1,0:T(8,128)S(1)} %get-tuple-element.305, pred[2048]{0:T(1024)(128)(4,1)S(1)} %fusion.113), kind=kOutput, calls=%fused_computation.7.clone.1 | convolution fusion | flops 1115684864 | bytes 36718592 | tf_op jit(solution)/shard_map/while/body/eval_jaxpr/hqk,khd->qhd/dot_general | solution.py:58
  269.2 0.3 bitcast_add_fusion.2
  269.5 15.7 %fusion.115 = f32[8,512]{1,0:T(8,128)S(1)} fusion(f32[8,2048,512]{2,1,0:T(8,128)} %get-tuple-element.275, f32[8,512]{1,0:T(8,128)S(1)} %get-tuple-element.305, pred[2048]{0:T(1024)(128)(4,1)S(1)} %fusion.113), kind=kLoop, calls=%fused_computation.6.clone.1 | loop fusion | flops 41938944 | bytes 33589248 | tf_op jit(solution)/shard_map/while/body/eval_jaxpr/reduce_sum | solution.py:57
  285.3 0.6 dynamic_slice.27
  286.6 4.5 constant_dynamic-slice_fusion.3
  291.0 4.0 copy.31
  295.1 15.6 %bitcast_reduce_fusion.2 = (f32[8,512]{1,0:T(8,128)S(1)}, f32[8,2048,512]{2,1,0:T(8,128)}) fusion(pred[2048]{0:T(1024)(128)(4,1)S(1)} %fusion.113, bf16[2048,8,64]{0,2,1:T(8,128)(2,1)} %bitcast.120, bf16[512,8,64]{0,2,1:T(8,128)(2,1)S(1)} %get-tuple-element.311), kind=kOutput, calls=%fused_computation.1.clone.1 | convolution fusion | flops 1098903552 | bytes 36194304 | tf_op jit(solution)/shard_map/while/body/eval_jaxpr/qhd,khd->hqk/dot_general | solution.py:50
  310.8 4.0 copy.32
  314.7 14.9 %fusion.117 = f32[8,64,512]{2,1,0:T(8,128)S(1)} fusion(bf16[2048,8,64]{0,2,1:T(8,128)(2,1)} %bitcast.121, f32[8,2048,512]{2,1,0:T(8,128)} %get-tuple-element.275, f32[8,512]{1,0:T(8,128)S(1)} %get-tuple-element.305, pred[2048]{0:T(1024)(128)(4,1)S(1)} %fusion.113), kind=kOutput, calls=%fused_computation.7.clone.1 | convolution fusion | flops 1115684864 | bytes 36718592 | tf_op jit(solution)/shard_map/while/body/eval_jaxpr/hqk,khd->qhd/dot_general | solution.py:58
  330.1 15.7 %fusion.115 = f32[8,512]{1,0:T(8,128)S(1)} fusion(f32[8,2048,512]{2,1,0:T(8,128)} %get-tuple-element.275, f32[8,512]{1,0:T(8,128)S(1)} %get-tuple-element.305, pred[2048]{0:T(1024)(128)(4,1)S(1)} %fusion.113), kind=kLoop, calls=%fused_computation.6.clone.1 | loop fusion | flops 41938944 | bytes 33589248 | tf_op jit(solution)/shard_map/while/body/eval_jaxpr/reduce_sum | solution.py:57
  345.8 0.6 dynamic_slice.27
  347.1 4.5 constant_dynamic-slice_fusion.3
  351.6 4.0 copy.31
  355.7 15.6 %bitcast_reduce_fusion.2 = (f32[8,512]{1,0:T(8,128)S(1)}, f32[8,2048,512]{2,1,0:T(8,128)}) fusion(pred[2048]{0:T(1024)(128)(4,1)S(1)} %fusion.113, bf16[2048,8,64]{0,2,1:T(8,128)(2,1)} %bitcast.120, bf16[512,8,64]{0,2,1:T(8,128)(2,1)S(1)} %get-tuple-element.311), kind=kOutput, calls=%fused_computation.1.clone.1 | convolution fusion | flops 1098903552 | bytes 36194304 | tf_op jit(solution)/shard_map/while/body/eval_jaxpr/qhd,khd->hqk/dot_general | solution.py:50
  371.3 4.0 copy.32
  375.3 14.9 %fusion.117 = f32[8,64,512]{2,1,0:T(8,128)S(1)} fusion(bf16[2048,8,64]{0,2,1:T(8,128)(2,1)} %bitcast.121, f32[8,2048,512]{2,1,0:T(8,128)} %get-tuple-element.275, f32[8,512]{1,0:T(8,128)S(1)} %get-tuple-element.305, pred[2048]{0:T(1024)(128)(4,1)S(1)} %fusion.113), kind=kOutput, calls=%fused_computation.7.clone.1 | convolution fusion | flops 1115684864 | bytes 36718592 | tf_op jit(solution)/shard_map/while/body/eval_jaxpr/hqk,khd->qhd/dot_general | solution.py:58
  390.2 0.3 bitcast_add_fusion.2
  390.6 15.7 %fusion.115 = f32[8,512]{1,0:T(8,128)S(1)} fusion(f32[8,2048,512]{2,1,0:T(8,128)} %get-tuple-element.275, f32[8,512]{1,0:T(8,128)S(1)} %get-tuple-element.305, pred[2048]{0:T(1024)(128)(4,1)S(1)} %fusion.113), kind=kLoop, calls=%fused_computation.6.clone.1 | loop fusion | flops 41938944 | bytes 33589248 | tf_op jit(solution)/shard_map/while/body/eval_jaxpr/reduce_sum | solution.py:57
  406.3 1.3 fusion.52
  407.7 2.9 convolution_convert_fusion.2
  410.9 38.6 %all-reduce.5.cloned.1.call-done = bf16[512,1024]{1,0:T(8,128)(2,1)} async-done(((bf16[512,1024]{1,0:T(8,128)(2,1)}), bf16[512,1024]{1,0:T(8,128)(2,1)}) %all-reduce.5.cloned.1.call-update) | async-done | bytes 1048592 | tf_op jit(solution)/shard_map/psum | solution.py:137
  449.5 2.0 multiply_reduce_fusion.1
  451.5 5.9 fusion.34
  457.4 7.9 %convolution_convert_fusion = bf16[512,1024]{1,0:T(8,128)(2,1)} fusion(bf16[1408,1024]{1,0:T(8,128)(2,1)S(1)} %copy-done, f32[512,1408]{1,0:T(8,128)} %fusion.34, bf16[2,1024,1408]{2,1,0:T(8,128)(2,1)} %param.24, bf16[512,1024]{1,0:T(8,128)(2,1)} %all-reduce.5.cloned.1.call-done, bf16[512,1024]{1,0:T(8,128)(2,1)} %param.19, f32[1024]{0:T(1024)S(1)} %copy-done.12, ...), kind=kOutput, calls=%fused_computation.77 | convolution fusion | flops 2963668992 | bytes 11802624 | tf_op jit(solution)/shard_map/dot_general | solution.py:74
  465.4 1.5 fusion.41
  467.0 2.4 convolution_convert_fusion.4
  469.4 36.1 %all-reduce.7.cloned.1.call-done = bf16[512,1024]{1,0:T(8,128)(2,1)} async-done(((bf16[512,1024]{1,0:T(8,128)(2,1)}), bf16[512,1024]{1,0:T(8,128)(2,1)}) %all-reduce.7.cloned.1.call-update) | async-done | bytes 1048592 | tf_op jit(solution)/shard_map/psum | solution.py:142
  505.5 2.6 multiply_reduce_fusion
  508.3 0.5 multiply_convert_fusion
  508.8 0.9 copy-done.10
  509.7 0.8 convolution_convert_fusion.3
  510.5 1.6 convolution_convert_fusion.5
  512.1 5.2 fusion.19
  517.2 61.0 %pmax.7 = f32[8,512]{1,0:T(8,128)S(1)} all-reduce(f32[8,512]{1,0:T(8,128)S(1)} %get-tuple-element.209), channel_id=1, replica_groups=mesh['seq'=16,'head'=2] {'seq'}, use_global_device_ids=true, to_apply=%region_13.14 | all-reduce | flops 4096 | bytes 32768 | tf_op jit(solution)/shard_map/pmax | solution.py:166
  578.2 6.4 fusion.45
  584.8 4.7 fusion.20
  589.4 30.1 %psum.38 = bf16[512,8]{0,1:T(8,128)(2,1)S(1)} all-reduce(bf16[512,8]{0,1:T(8,128)(2,1)S(1)} %bitcast.127), channel_id=1, replica_groups=mesh['seq'=16,'head'=2] {'seq'}, use_global_device_ids=true, to_apply=%region_16.17 | all-reduce | flops 4096 | bytes 16384 | tf_op jit(solution)/shard_map/psum | solution.py:178
  619.6 52.5 %all-reduce.9.cloned.1.call-done = bf16[512,512]{0,1:T(8,128)(2,1)} async-done(((bf16[512,512]{0,1:T(8,128)(2,1)}), bf16[512,512]{0,1:T(8,128)(2,1)}) %all-reduce.9.cloned.1.call-update) | async-done | bytes 524304 | tf_op jit(solution)/shard_map/psum | solution.py:179
  672.1 1.1 fusion.49
  673.2 2.9 convolution_convert_fusion.1
  676.2 0.7 fusion.85
  676.9 2.5 compare_select_fusion.1
  679.4 37.5 %all-reduce.11.cloned.1.call-done = bf16[512,1024]{1,0:T(8,128)(2,1)} async-done(((bf16[512,1024]{1,0:T(8,128)(2,1)}), bf16[512,1024]{1,0:T(8,128)(2,1)}) %all-reduce.11.cloned.1.call-update) | async-done | bytes 1048592 | tf_op jit(solution)/shard_map/psum | solution.py:185
  716.9 2.9 fusion.44
  (91 shorter events, 1.9 us)
Async XLA Ops:
  7.2 450.2 %copy-start = (bf16[1408,1024]{1,0:T(8,128)(2,1)S(1)}, bf16[1408,1024]{1,0:T(8,128)(2,1)}, u32[]{:S(2)}) copy-start(bf16[1408,1024]{1,0:T(8,128)(2,1)} %param.25) | copy-start | bytes 8650756
  7.2 4.9 copy-start.11
  7.2 82.0 %all-gather.3.cloned.1.call-start = ((), (), s32[]{:S(2)}) async-start(), calls=%async_computation | async-start | bytes 8912896 | tf_op jit(solution)/shard_map/all_gather | solution.py:111
  12.0 152.3 %all-gather.5.cloned.1.call-start = ((), (), s32[]{:S(2)}) async-start(), calls=%async_computation.1 | async-start | bytes 8912896 | tf_op jit(solution)/shard_map/all_gather | solution.py:112
  15.2 149.1 %copy-start.7 = (s32[16]{0:T(128)S(1)}, s32[16]{0:T(128)}, u32[]{:S(2)}) copy-start(s32[16]{0:T(128)} %param.27) | copy-start | bytes 196
  15.2 434.3 %all-reduce.5.cloned.1.call-start = ((), (), s32[]{:S(2)}) async-start(), calls=%async_computation.2 | async-start | bytes 2097152 | tf_op jit(solution)/shard_map/psum | solution.py:137
  193.7 14.9 %copy-start.1 = (f32[512,512]{0,1:T(8,128)S(1)}, f32[512,512]{0,1:T(8,128)}, u32[]{:S(2)}) copy-start(f32[512,512]{0,1:T(8,128)} %get-tuple-element.294) | copy-start | bytes 3145732 | tf_op jit(solution)/shard_map/while
  209.0 15.7 %copy-start.2 = (f32[512,512]{0,1:T(8,128)}, f32[512,512]{0,1:T(8,128)S(1)}, u32[]{:S(2)}) copy-start(f32[512,512]{0,1:T(8,128)S(1)} %bitcast_add_fusion.2) | copy-start | bytes 3145732 | tf_op jit(solution)/shard_map/while
  254.2 14.9 %copy-start.1 = (f32[512,512]{0,1:T(8,128)S(1)}, f32[512,512]{0,1:T(8,128)}, u32[]{:S(2)}) copy-start(f32[512,512]{0,1:T(8,128)} %get-tuple-element.294) | copy-start | bytes 3145732 | tf_op jit(solution)/shard_map/while
  269.5 15.7 %copy-start.2 = (f32[512,512]{0,1:T(8,128)}, f32[512,512]{0,1:T(8,128)S(1)}, u32[]{:S(2)}) copy-start(f32[512,512]{0,1:T(8,128)S(1)} %bitcast_add_fusion.2) | copy-start | bytes 3145732 | tf_op jit(solution)/shard_map/while
  314.7 14.9 %copy-start.1 = (f32[512,512]{0,1:T(8,128)S(1)}, f32[512,512]{0,1:T(8,128)}, u32[]{:S(2)}) copy-start(f32[512,512]{0,1:T(8,128)} %get-tuple-element.294) | copy-start | bytes 3145732 | tf_op jit(solution)/shard_map/while
  330.0 15.7 %copy-start.2 = (f32[512,512]{0,1:T(8,128)}, f32[512,512]{0,1:T(8,128)S(1)}, u32[]{:S(2)}) copy-start(f32[512,512]{0,1:T(8,128)S(1)} %bitcast_add_fusion.2) | copy-start | bytes 3145732 | tf_op jit(solution)/shard_map/while
  375.3 14.9 %copy-start.1 = (f32[512,512]{0,1:T(8,128)S(1)}, f32[512,512]{0,1:T(8,128)}, u32[]{:S(2)}) copy-start(f32[512,512]{0,1:T(8,128)} %get-tuple-element.294) | copy-start | bytes 3145732 | tf_op jit(solution)/shard_map/while
  390.6 15.7 %copy-start.2 = (f32[512,512]{0,1:T(8,128)}, f32[512,512]{0,1:T(8,128)S(1)}, u32[]{:S(2)}) copy-start(f32[512,512]{0,1:T(8,128)S(1)} %bitcast_add_fusion.2) | copy-start | bytes 3145732 | tf_op jit(solution)/shard_map/while
  407.7 43.8 %copy-start.12 = (f32[1024]{0:T(1024)S(1)}, f32[1024]{0:T(1024)}, u32[]{:S(2)}) copy-start(f32[1024]{0:T(1024)} %param.23) | copy-start | bytes 12292
  410.6 94.9 %all-reduce.7.cloned.1.call-start = ((), (), s32[]{:S(2)}) async-start(), calls=%async_computation.3 | async-start | bytes 2097152 | tf_op jit(solution)/shard_map/psum | solution.py:142
  457.4 9.6 %copy-start.13 = (f32[1024]{0:T(1024)S(1)}, f32[1024]{0:T(1024)}, u32[]{:S(2)}) copy-start(f32[1024]{0:T(1024)} %param.30) | copy-start | bytes 12292
  465.3 206.8 %all-reduce.9.cloned.1.call-start = ((), (), s32[]{:S(2)}) async-start(), calls=%async_computation.4 | async-start | bytes 1048576 | tf_op jit(solution)/shard_map/psum | solution.py:179
  467.0 41.1 %copy-start.9 = (f32[1024]{0:T(1024)S(1)}, f32[1024]{0:T(1024)}, u32[]{:S(2)}) copy-start(f32[1024]{0:T(1024)} %param.26) | copy-start | bytes 12292
  505.5 2.6 copy-start.3
  505.5 2.6 copy-start.4
  505.5 2.8 copy-start.5
  508.1 1.7 copy-start.10
  509.7 2.3 copy-start.6
  584.7 132.2 %all-reduce.11.cloned.1.call-start = ((), (), s32[]{:S(2)}) async-start(), calls=%async_computation.5 | async-start | bytes 2097152 | tf_op jit(solution)/shard_map/psum | solution.py:185
  589.4 86.8 %copy-start.8 = (s32[4]{0:T(128)S(1)}, s32[4]{0:T(128)}, u32[]{:S(2)}) copy-start(s32[4]{0:T(128)} %param.29) | copy-start | bytes 52
Sparse Core Ops, SparseCore 0:
  12.2 77.0 all-gather.2
  91.4 72.8 all-gather.4
  410.8 38.6 all-reduce.4
  465.4 40.0 all-reduce.6
  584.8 87.1 all-reduce.8
  676.3 40.5 all-reduce.10
where the time goes:
time: 728 us; the launch traced here: 727 us
  waiting for transfers between devices  311 us (43%)
  matrix products  167 us (23%)
  blocking collectives  91.1 us (13%)
  other arithmetic  85.7 us (12%)
  local copies, waits for them, and re-layouts  53.9 us (7%)
  between operations  14.4 us (2%)
    all_gather x1, waiting for transfers between devices, local(): value_piece = lax.all_gather(values_local, 'seq', axis=0, tiled=True)  75.1 us
    all_gather x1, waiting for transfers between devices, local(): key_piece = lax.all_gather(keys_local, 'seq', axis=0, tiled=True)  71.5 us
    reduce_sum x4, other arithmetic, flash_block(): new_sum = running_sum * shrink + jnp.sum(weights, axis=-1)  62.8 us
    dot_general x4, matrix products, flash_block(): jnp.einsum('qhd,khd->hqk', query_heads, keys_split, preferred_element_typ...  62.5 us
    pmax x1, blocking collectives, local(): global_max = lax.pmax(local_max, 'seq')  61 us
    dot_general x4, matrix products, flash_block(): jnp.einsum('hqk,khd->qhd', weights.astype(jnp.bfloat16), values_split, pr...  59.7 us
    psum x1, waiting for transfers between devices, local(): lax.psum(local_mixed.reshape(target_rows, heads_here * HD).astype(jnp.bfl...  52.5 us
    psum x1, waiting for transfers between devices, local(): lax.psum(attn_part.astype(jnp.bfloat16), 'head').astype(jnp.float32)  38.6 us
  transfers between devices with their start and end apart: 6, of which 6 were waited for; matrix products, arithmetic and copies ran while one was open for 2% of the time, Pallas kernels for 0%

commit v1 on v0

v1 whole, which is shorter than its diff:
```python
import functools
import math

import jax
import jax.numpy as jnp
from jax import lax
from jax.experimental import pallas as pl
from jax.experimental.pallas import tpu as pltpu
from jax.sharding import PartitionSpec as P

HD = 64
TOK_DEV = 512
TGT_LEN = 128

epsilon = 1e-06
masked_score = -1e30
MESH = pl.DeviceIdType.MESH


def rms_norm(values, gain_vector):
    widened = values.astype(jnp.float32)
    return (
        widened
        * lax.rsqrt(jnp.mean(widened * widened, axis=-1, keepdims=True) + epsilon)
        * gain_vector
    )


def spread_heads(per_head):
    return jnp.repeat(per_head.T, HD, axis=1)


def greet_all(me, ring):
    barrier = pltpu.get_barrier_semaphore()

    def greet(i, carry):
        pl.semaphore_signal(
            barrier, inc=1, device_id={"seq": lax.rem(me + i, ring)}, device_id_type=MESH
        )
        return carry

    lax.fori_loop(1, ring, greet, 0)
    pl.semaphore_wait(barrier, ring - 1)


def scatter_kernel(ring, share, q_in, kv_in, q_out, kv_out, qs, qr, ks, kr, fs, fr, ls):
    me = lax.axis_index("seq")
    part = kv_in.shape[1]
    mine = pl.ds(pl.multiple_of(lax.rem(me, share) * part, part), part)
    own_q = pltpu.make_async_copy(q_in.at[me], q_out.at[me], ls.at[0])
    own_kv = pltpu.make_async_copy(kv_in.at[me], kv_out.at[me, mine], ls.at[1])
    own_q.start()
    own_kv.start()
    greet_all(me, ring)

    def q_copy(i):
        to = lax.rem(me + i, ring)
        return pltpu.make_async_remote_copy(
            src_ref=q_in.at[to],
            dst_ref=q_out.at[me],
            send_sem=qs.at[i],
            recv_sem=qr.at[i],
            device_id={"seq": to},
            device_id_type=MESH,
        )

    def kv_copy(i):
        to = lax.rem(me + i, ring)
        rows = pl.ds(pl.multiple_of(lax.rem(to, share) * part, part), part)
        return pltpu.make_async_remote_copy(
            src_ref=kv_in.at[to],
            dst_ref=kv_out.at[me, rows],
            send_sem=ks.at[i],
            recv_sem=kr.at[i],
            device_id={"seq": to},
            device_id_type=MESH,
        )

    def forward(i, k):
        origin = lax.rem(me - i + ring, ring)
        slot = lax.rem(me, share)
        to = me - slot + lax.rem(slot + k, share)
        block = kv_out.at[origin, mine]
        return pltpu.make_async_remote_copy(
            src_ref=block,
            dst_ref=block,
            send_sem=fs.at[i, k],
            recv_sem=fr.at[i, k],
            device_id={"seq": to},
            device_id_type=MESH,
        )

    def arrived(i, k):
        slot = lax.rem(me, share)
        giver = me - slot + lax.rem(slot - k + share, share)
        origin = lax.rem(giver - i + ring, ring)
        rows = pl.ds(pl.multiple_of(lax.rem(giver, share) * part, part), part)
        block = kv_out.at[origin, rows]
        return pltpu.make_async_remote_copy(
            src_ref=block,
            dst_ref=block,
            send_sem=fs.at[i, k],
            recv_sem=fr.at[i, k],
            device_id={"seq": giver},
            device_id_type=MESH,
        )

    def send(i, carry):
        kv_copy(i).start()
        q_copy(i).start()
        return carry

    lax.fori_loop(1, ring, send, 0)
    own_kv.wait()
    for k in range(1, share):
        forward(0, k).start()

    def relay(i, carry):
        pltpu.make_async_remote_copy(
            src_ref=kv_in.at[0],
            dst_ref=kv_out.at[lax.rem(me - i + ring, ring), mine],
            send_sem=ks.at[i],
            recv_sem=kr.at[i],
            device_id={"seq": lax.rem(me + i, ring)},
            device_id_type=MESH,
        ).wait_recv()
        for k in range(1, share):
            forward(i, k).start()
        return carry

    lax.fori_loop(1, ring, relay, 0)

    def finish(i, carry):
        pltpu.make_async_remote_copy(
            src_ref=q_in.at[0],
            dst_ref=q_out.at[lax.rem(me - i + ring, ring)],
            send_sem=qs.at[i],
            recv_sem=qr.at[i],
            device_id={"seq": lax.rem(me + i, ring)},
            device_id_type=MESH,
        ).wait_recv()
        q_copy(i).wait_send()
        kv_copy(i).wait_send()
        return carry

    lax.fori_loop(1, ring, finish, 0)

    def drain(i, carry):
        for k in range(1, share):
            arrived(i, k).wait_recv()
            forward(i, k).wait_send()
        return carry

    lax.fori_loop(0, ring, drain, 0)
    own_q.wait()


def scatter_heads(ring, share, q_send, kv_send):
    part = kv_send.shape[1]
    return pl.pallas_call(
        functools.partial(scatter_kernel, ring, share),
        out_shape=(
            jax.ShapeDtypeStruct(q_send.shape, q_send.dtype),
            jax.ShapeDtypeStruct((ring, part * share, 2 * HD), kv_send.dtype),
        ),
        in_specs=[pl.BlockSpec(memory_space=pltpu.VMEM)] * 2,
        out_specs=(pl.BlockSpec(memory_space=pltpu.VMEM),) * 2,
        scratch_shapes=[
            pltpu.SemaphoreType.DMA((ring,)),
            pltpu.SemaphoreType.DMA((ring,)),
            pltpu.SemaphoreType.DMA((ring,)),
            pltpu.SemaphoreType.DMA((ring,)),
            pltpu.SemaphoreType.DMA((ring, share)),
            pltpu.SemaphoreType.DMA((ring, share)),
            pltpu.SemaphoreType.DMA((2,)),
        ],
        compiler_params=pltpu.CompilerParams(collective_id=0, has_side_effects=True),
        name="scatter_heads",
    )(q_send, kv_send)


def exchange_kernel(ring, x_in, x_out, ss, rs, ls):
    me = lax.axis_index("seq")
    own = pltpu.make_async_copy(x_in.at[me], x_out.at[me], ls)
    own.start()
    greet_all(me, ring)

    def outgoing(i):
        to = lax.rem(me + i, ring)
        return pltpu.make_async_remote_copy(
            src_ref=x_in.at[to],
            dst_ref=x_out.at[me],
            send_sem=ss.at[i],
            recv_sem=rs.at[i],
            device_id={"seq": to},
            device_id_type=MESH,
        )

    def send(i, carry):
        outgoing(i).start()
        return carry

    lax.fori_loop(1, ring, send, 0)

    def finish(i, carry):
        pltpu.make_async_remote_copy(
            src_ref=x_in.at[0],
            dst_ref=x_out.at[lax.rem(me - i + ring, ring)],
            send_sem=ss.at[i],
            recv_sem=rs.at[i],
            device_id={"seq": lax.rem(me + i, ring)},
            device_id_type=MESH,
        ).wait_recv()
        outgoing(i).wait_send()
        return carry

    lax.fori_loop(1, ring, finish, 0)
    own.wait()


def exchange(ring, blocks, which):
    return pl.pallas_call(
        functools.partial(exchange_kernel, ring),
        out_shape=jax.ShapeDtypeStruct(blocks.shape, blocks.dtype),
        in_specs=[pl.BlockSpec(memory_space=pltpu.VMEM)],
        out_specs=pl.BlockSpec(memory_space=pltpu.VMEM),
        scratch_shapes=[
            pltpu.SemaphoreType.DMA((ring,)),
            pltpu.SemaphoreType.DMA((ring,)),
            pltpu.SemaphoreType.DMA,
        ],
        compiler_params=pltpu.CompilerParams(collective_id=which, has_side_effects=True),
        name=f"exchange_{which}",
    )(blocks)


def attend_kernel(lengths, q_ref, kv_ref, o_ref, keys, values, count):
    blocks, span, lanes = kv_ref.shape
    tile = span
    queries = q_ref.shape[1]
    lane = lax.broadcasted_iota(jnp.int32, (span, lanes), 1)
    row = lax.broadcasted_iota(jnp.int32, (span, lanes), 0)

    @pl.when(pl.program_id(0) == 0)
    def pack():
        def place(j, start):
            block = kv_ref[j]
            dead = jnp.where(row < lengths[j], 0.0, masked_score).astype(jnp.bfloat16)
            at = pl.ds(pl.multiple_of(start, 16), span)
            keys[at, :] = jnp.where(lane < HD, block, dead)
            values[at, :] = jnp.where(lane < HD, jnp.ones_like(block), block)
            return start + ((lengths[j] + 15) // 16) * 16

        stop = lax.fori_loop(0, blocks, place, 0)
        at = pl.ds(pl.multiple_of(stop, 16), span)
        keys[at, :] = jnp.where(lane < HD, 0.0, masked_score).astype(jnp.bfloat16)
        values[at, :] = jnp.zeros((span, lanes), jnp.bfloat16)
        count[0] = (stop + tile - 1) // tile

    spare = lax.broadcasted_iota(jnp.int32, (HD, queries), 0)
    pick = jnp.where(spare == 0, 1.0, 0.0).astype(jnp.bfloat16)
    q_wide = jnp.concatenate([q_ref[...], pick], axis=0)

    def step(t, state):
        top, mixed = state
        at = pl.ds(pl.multiple_of(t * tile, tile), tile)
        scores = lax.dot_general(
            keys[at, :], q_wide, (((1,), (0,)), ((), ())), preferred_element_type=jnp.float32
        )
        new_top = jnp.maximum(top, jnp.max(scores, axis=0, keepdims=True))
        weights = jnp.exp(scores - new_top).astype(jnp.bfloat16)
        part = lax.dot_general(
            values[at, :], weights, (((0,), (0,)), ((), ())), preferred_element_type=jnp.float32
        )
        return new_top, mixed * jnp.exp(top - new_top) + part

    top, mixed = lax.fori_loop(
        0,
        count[0],
        step,
        (
            jnp.full((1, queries), masked_score, jnp.float32),
            jnp.zeros((lanes, queries), jnp.float32),
        ),
    )
    o_ref[...] = (mixed[HD:, :] / mixed[0:1, :]).astype(jnp.bfloat16)


def attend(q_all, kv_all, pad_lengths):
    blocks, span, lanes = kv_all.shape
    total = q_all.shape[1]
    width = math.gcd(total, 512)
    return pl.pallas_call(
        attend_kernel,
        out_shape=jax.ShapeDtypeStruct((HD, total), jnp.bfloat16),
        grid_spec=pltpu.PrefetchScalarGridSpec(
            num_scalar_prefetch=1,
            grid=(total // width,),
            in_specs=[
                pl.BlockSpec((HD, width), lambda i, lengths: (0, i)),
                pl.BlockSpec((blocks, span, lanes), lambda i, lengths: (0, 0, 0)),
            ],
            out_specs=pl.BlockSpec((HD, width), lambda i, lengths: (0, i)),
            scratch_shapes=[
                pltpu.VMEM(((blocks + 1) * span, lanes), jnp.bfloat16),
                pltpu.VMEM(((blocks + 1) * span, lanes), jnp.bfloat16),
                pltpu.SMEM((1,), jnp.int32),
            ],
        ),
        compiler_params=pltpu.CompilerParams(
            dimension_semantics=("arbitrary",), vmem_limit_bytes=40 * 1024 * 1024
        ),
        name="attend",
    )(pad_lengths, q_all, kv_all)


def feed_forward(normed_in, ffn_in, ffn_out):
    gate_proj = jnp.dot(normed_in, ffn_in[0], preferred_element_type=jnp.float32)
    up_proj = jnp.dot(normed_in, ffn_in[1], preferred_element_type=jnp.float32)
    activated = (jax.nn.gelu(gate_proj, approximate=True) * up_proj).astype(jnp.bfloat16)
    return jnp.dot(activated, ffn_out, preferred_element_type=jnp.float32)


def local(
    ring,
    tokens,
    norm_attn,
    self_qkv,
    self_out,
    norm_ffn,
    ffn_in,
    ffn_out,
    norm_final,
    pad_lengths,
    targets,
    target_lengths,
    norm_cross,
    cross_query,
    cross_kv,
    cross_out,
):
    row_count = tokens.shape[0]
    heads_here = self_qkv.shape[2] // HD
    share = ring // heads_here
    part = row_count // share
    scaling = HD ** (-0.5)
    normed = rms_norm(tokens, norm_attn).astype(jnp.bfloat16)
    q_t = lax.dot_general(
        self_qkv[0], normed, (((0,), (1,)), ((), ())), preferred_element_type=jnp.float32
    ).astype(jnp.bfloat16) * jnp.bfloat16(scaling)
    keys_local = jnp.dot(normed, self_qkv[1], preferred_element_type=jnp.float32).astype(
        jnp.bfloat16
    )
    values_local = jnp.dot(normed, self_qkv[2], preferred_element_type=jnp.float32).astype(
        jnp.bfloat16
    )
    q_send = (
        q_t.reshape(heads_here, HD, share, part).transpose(0, 2, 1, 3).reshape(ring, HD, part)
    )
    kv_local = jnp.concatenate(
        [
            keys_local.reshape(row_count, heads_here, HD),
            values_local.reshape(row_count, heads_here, HD),
        ],
        axis=2,
    )
    kv_send = kv_local.transpose(1, 0, 2).reshape(ring, part, 2 * HD)
    q_got, kv_got = scatter_heads(ring, share, q_send, kv_send)
    q_all = q_got.transpose(1, 0, 2).reshape(HD, ring * part)
    mixed_t = attend(q_all, kv_got, pad_lengths)
    back = mixed_t.reshape(HD, ring, part).transpose(1, 0, 2)
    context_t = (
        exchange(ring, back, 1)
        .reshape(heads_here, share, HD, part)
        .transpose(0, 2, 1, 3)
        .reshape(heads_here * HD, row_count)
    )
    attn_part = lax.dot_general(
        context_t, self_out, (((0,), (0,)), ((), ())), preferred_element_type=jnp.float32
    )
    hidden_in = tokens.astype(jnp.float32) + lax.psum(
        attn_part.astype(jnp.bfloat16), "head"
    ).astype(jnp.float32)
    ffn_normed = rms_norm(hidden_in, norm_ffn).astype(jnp.bfloat16)
    ffn_part = feed_forward(ffn_normed, ffn_in, ffn_out)
    final_in = hidden_in + lax.psum(ffn_part.astype(jnp.bfloat16), "head").astype(jnp.float32)
    encoded = rms_norm(final_in, norm_final).astype(jnp.bfloat16)
    target_rows = targets.shape[0]
    cross_normed = rms_norm(targets, norm_cross).astype(jnp.bfloat16)
    cross_q_t = lax.dot_general(
        cross_query, cross_normed, (((0,), (1,)), ((), ())), preferred_element_type=jnp.float32
    ).astype(jnp.bfloat16) * jnp.bfloat16(scaling)
    cross_keys = jnp.dot(encoded, cross_kv[0], preferred_element_type=jnp.float32).astype(
        jnp.bfloat16
    )
    cross_values = jnp.dot(encoded, cross_kv[1], preferred_element_type=jnp.float32).astype(
        jnp.bfloat16
    )
    my_length = lax.dynamic_slice_in_dim(pad_lengths, lax.axis_index("seq"), 1, 0)
    mixed, top = cross_attend(my_length, cross_q_t, cross_keys, cross_values)
    slice_rows = target_rows // ring
    sent = (
        mixed.reshape(heads_here, 2 * HD, ring, slice_rows)
        .transpose(2, 0, 1, 3)
        .reshape(ring, heads_here * 2 * HD * slice_rows // 512, 512)
    )
    got = exchange(ring, sent, 2).reshape(ring, heads_here, 2 * HD, slice_rows)
    tops = exchange(
        ring,
        jnp.broadcast_to(
            top.reshape(heads_here, 1, ring, slice_rows)
            .transpose(2, 0, 1, 3)
            .reshape(ring, heads_here, slice_rows),
            (ring, heads_here, slice_rows),
        ),
        3,
    ).reshape(ring, heads_here, 1, slice_rows)
    best = jnp.max(tops, axis=0, keepdims=True)
    summed = jnp.sum(got.astype(jnp.float32) * jnp.exp(tops - best), axis=0)
    cross_context = (summed[:, HD:, :] / summed[:, 0:1, :]).astype(jnp.bfloat16)
    cross_context = cross_context.reshape(heads_here * HD, slice_rows)
    cross_part = lax.dot_general(
        cross_context, cross_out, (((0,), (0,)), ((), ())), preferred_element_type=jnp.float32
    )
    cross_total = lax.psum(cross_part.astype(jnp.bfloat16), "head").astype(jnp.float32)
    slots = lax.axis_index("seq") * slice_rows + jnp.arange(slice_rows, dtype=jnp.int32)
    owner = slots // TGT_LEN
    limits = jnp.sum(
        jnp.where(
            owner[:, None] == jnp.arange(target_lengths.shape[0])[None, :],
            target_lengths[None, :],
            0,
        ),
        axis=1,
    )
    target_live = slots % TGT_LEN < limits
    mine = lax.dynamic_slice_in_dim(targets, lax.axis_index("seq") * slice_rows, slice_rows, 0)
    decoded_here = (
        mine.astype(jnp.float32) + jnp.where(target_live[:, None], cross_total, 0.0)
    ).astype(jnp.bfloat16)
    decoded = lax.all_gather(decoded_here, "seq", axis=0, tiled=True)
    return (encoded, decoded)


def cross_kernel(length, q_ref, k_ref, v_ref, o_ref, top_ref):
    rows = k_ref.shape[0]
    queries = q_ref.shape[1]
    live = lax.broadcasted_iota(jnp.int32, (rows, queries), 0) < length[0]
    lane = lax.broadcasted_iota(jnp.int32, (rows, 2 * HD), 1)
    ones = jnp.ones((rows, 2 * HD), jnp.bfloat16)
    for h in range(2):
        own = lane < HD if h == 0 else lane >= HD
        keys = jnp.where(own, k_ref[...], jnp.zeros_like(ones))
        values = jnp.where(own, v_ref[...], ones)
        scores = lax.dot_general(
            keys, q_ref[...], (((1,), (0,)), ((), ())), preferred_element_type=jnp.float32
        )
        scores = jnp.where(live, scores, masked_score)
        top = jnp.max(scores, axis=0, keepdims=True)
        weights = jnp.exp(scores - top).astype(jnp.bfloat16)
        part = lax.dot_general(
            values, weights, (((0,), (0,)), ((), ())), preferred_element_type=jnp.float32
        ).astype(jnp.bfloat16)
        if h == 0:
            o_ref[0, :HD, :] = part[HD:, :]
            o_ref[0, HD:, :] = part[:HD, :]
        else:
            o_ref[1] = part
        top_ref[h] = top


def cross_attend(my_length, q_t, keys, values):
    rows, width = keys.shape
    queries = q_t.shape[1]
    heads = width // HD
    return pl.pallas_call(
        cross_kernel,
        out_shape=(
            jax.ShapeDtypeStruct((heads, 2 * HD, queries), jnp.bfloat16),
            jax.ShapeDtypeStruct((heads, 1, queries), jnp.float32),
        ),
        grid_spec=pltpu.PrefetchScalarGridSpec(
            num_scalar_prefetch=1,
            grid=(heads // 2,),
            in_specs=[
                pl.BlockSpec((2 * HD, queries), lambda i, n: (i, 0)),
                pl.BlockSpec((rows, 2 * HD), lambda i, n: (0, i)),
                pl.BlockSpec((rows, 2 * HD), lambda i, n: (0, i)),
            ],
            out_specs=(
                pl.BlockSpec((2, 2 * HD, queries), lambda i, n: (i, 0, 0)),
                pl.BlockSpec((2, 1, queries), lambda i, n: (i, 0, 0)),
            ),
        ),
        compiler_params=pltpu.CompilerParams(vmem_limit_bytes=32 * 1024 * 1024),
        name="cross_attend",
    )(my_length, q_t, keys, values)


def solution(mesh):
    ring = mesh.shape["seq"]
    placed = (
        P("seq", None),
        P(),
        P(None, None, "head"),
        P("head", None),
        P(),
        P(None, None, "head"),
        P("head", None),
        P(),
        P(),
        P(),
        P(),
        P(),
        P(None, "head"),
        P(None, None, "head"),
        P("head", None),
    )
    return jax.shard_map(
        functools.partial(local, ring),
        mesh=mesh,
        in_specs=placed,
        out_specs=(P("seq", None), P()),
        check_vma=False,
    )
```

time: 728 us -> 397 us (0.55)
  waiting for transfers between devices: 311 us -> 144 us
  Pallas kernels: 0 us -> 151 us
  matrix products: 167 us -> 26.7 us
  blocking collectives: 91.1 us -> 0 us
  other arithmetic: 85.7 us -> 17.2 us
  local copies, waits for them, and re-layouts: 53.9 us -> 42 us
    pallas_call x0 -> x6, Pallas kernels: none -> 151 us  [the longest x3 57.1 us: exchange(): pl.pallas_call(functools.partial(exchange_kernel, ring), out_shape=jax.Sh...]
    dot_general x14 -> x4, matrix products: 144 us -> 7.91 us  [the longest x1 2.39 us: local(): lax.dot_general(cross_query, cross_normed, (((0,), (1,)), ((), ())), pref...]
    all_gather x2 -> x1, waiting for transfers between devices: 147 us -> 38.9 us  [local(): decoded = lax.all_gather(decoded_here, 'seq', axis=0, tiled=True)]
    reduce_sum x10 -> x2, other arithmetic: 68 us -> 2.28 us  [the longest x1 2.2 us: local(): summed = jnp.sum(got.astype(jnp.float32) * jnp.exp(tops - best), axis=0)]
    pmax x1 -> x0, blocking collectives: 61 us -> none  [local(): global_max = lax.pmax(local_max, 'seq')]
    psum x1 -> x0, waiting for transfers between devices: 52.5 us -> none  [local(): lax.psum(local_mixed.reshape(target_rows, heads_here * HD).astype(jnp.bfl...]
    dynamic_slice x16 -> x1, local copies, waits for them, and re-layouts: 52 us -> 0.59 us  [local(): lax.dynamic_slice_in_dim(pad_lengths, lax.axis_index('seq'), 1, 0)]
    psum x1 -> x0, blocking collectives: 30.1 us -> none  [local(): lax.psum(local_sum.astype(jnp.bfloat16), 'seq').astype(jnp.float32)]
  transfers between devices with their start and end apart: 6 -> 4, of which waited for: 6 -> 4; matrix products, arithmetic and copies ran while one was open for 2% -> 1% of each run, Pallas kernels for 0% -> 0%
where the time goes in v1:
time: 397 us; the launch traced here: 396 us
  Pallas kernels  151 us (38%)
  waiting for transfers between devices  144 us (36%)
  local copies, waits for them, and re-layouts  42 us (11%)
  matrix products  26.7 us (7%)
  other arithmetic  17.2 us (4%)
  between operations  14.1 us (4%)
    pallas_call x3, Pallas kernels, exchange(): pl.pallas_call(functools.partial(exchange_kernel, ring), out_shape=jax.Sh...  57.1 us
    pallas_call x1, Pallas kernels, attend(): pl.pallas_call(attend_kernel, out_shape=jax.ShapeDtypeStruct((HD, total),...  52.8 us
    psum x1, waiting for transfers between devices, local(): lax.psum(attn_part.astype(jnp.bfloat16), 'head').astype(jnp.float32)  43.7 us
    all_gather x1, waiting for transfers between devices, local(): decoded = lax.all_gather(decoded_here, 'seq', axis=0, tiled=True)  38.9 us
    pallas_call x1, Pallas kernels, scatter_heads(): pl.pallas_call(functools.partial(scatter_kernel, ring, share), out_shape=...  36.2 us
    psum x1, waiting for transfers between devices, local(): lax.psum(ffn_part.astype(jnp.bfloat16), 'head').astype(jnp.float32)  35.4 us
    psum x1, waiting for transfers between devices, local(): lax.psum(cross_part.astype(jnp.bfloat16), 'head').astype(jnp.float32)  26.2 us
    mul x2, local copies, waits for them, and re-layouts, local(): summed = jnp.sum(got.astype(jnp.float32) * jnp.exp(tops - best), axis=0)  11.1 us
  transfers between devices with their start and end apart: 4, of which 4 were waited for; matrix products, arithmetic and copies ran while one was open for 1% of the time, Pallas kernels for 0%

profile of v1, /device:TPU:0, one launch (start us, length us, event | category | flops | bytes accessed | tf_op | source)
XLA Modules:
  0.0 395.9 jit_solution(1131928467767903875)
XLA Ops:
  7.2 0.0 copy-start
  7.2 0.0 all-reduce.4.cloned.1.call-start
  7.2 1.7 fusion.16
  8.9 3.3 convolution_convert_fusion.6
  12.3 0.9 convolution_convert_fusion.5
  13.1 1.6 fusion.20
  14.8 2.4 copy.37
  17.2 1.3 copy.38
  18.5 1.2 reshape.130
  19.6 0.9 copy.36
  20.5 3.1 pad_maximum_fusion
  23.6 36.2 %scatter_heads.1 = (bf16[16,64,256]{2,1,0:T(8,128)(2,1)}, bf16[16,512,128]{2,1,0:T(8,128)(2,1)}) custom-call(bf16[16,64,256]{2,1,0:T(8,128)(2,1)} %bitcast.75, bf16[16,256,128]{2,1,0:T(8,128)(2,1)} %bitcast.73), custom_call_target="tpu_custom_call" | custom-call | tf_op jit(solution)/shard_map/scatter_heads/pallas_call | solution.py:160
  59.8 1.1 copy.49
  60.9 1.6 copy-done.1
  62.5 52.8 %attend.1 = bf16[64,4096]{1,0:T(8,128)(2,1)S(1)} custom-call(s32[16]{0:T(128)S(1)} %copy-done.3, bf16[64,4096]{1,0:T(8,128)(2,1)S(1)} %bitcast.71, bf16[16,512,128]{2,1,0:T(8,128)(2,1)S(1)} %copy-done.1), custom_call_target="tpu_custom_call" | custom-call | tf_op jit(solution)/shard_map/attend/pallas_call | solution.py:293
  115.3 0.8 copy.53
  116.1 24.3 %exchange_1.1 = bf16[16,64,256]{2,1,0:T(8,128)(2,1)} custom-call(bf16[16,64,256]{2,1,0:T(8,128)(2,1)} %bitcast.77), custom_call_target="tpu_custom_call" | custom-call | tf_op jit(solution)/shard_map/exchange_1/pallas_call | solution.py:222
  140.5 1.7 copy.41
  142.2 0.1 copy.50
  142.3 1.7 convolution_convert_fusion.1
  144.0 0.0 all-reduce.4.cloned.1.call-update
  144.0 0.0 all-reduce.6.cloned.1.call-start
  144.0 43.7 %all-reduce.4.cloned.1.call-done = bf16[512,1024]{1,0:T(8,128)(2,1)} async-done(((bf16[512,1024]{1,0:T(8,128)(2,1)}), bf16[512,1024]{1,0:T(8,128)(2,1)}) %all-reduce.4.cloned.1.call-update) | async-done | bytes 1048592 | tf_op jit(solution)/shard_map/psum | solution.py:381
  187.7 2.1 multiply_reduce_fusion.2
  189.8 0.0 copy-done.7
  189.9 5.3 %fusion.9 = f32[512,1408]{1,0:T(8,128)} fusion(bf16[2,1024,1408]{2,1,0:T(8,128)(2,1)} %param.20, bf16[512,1024]{1,0:T(8,128)(2,1)S(1)} %copy-done.7, bf16[512,1024]{1,0:T(8,128)(2,1)S(1)} %copy-done.5, f32[1024]{0:T(1024)S(1)} %copy-done.16, f32[512]{0:T(512)S(1)} %add_rsqrt_fusion.2), kind=kOutput, calls=%fused_computation.14 | convolution fusion | flops 1479540736 | bytes 7870464 | tf_op jit(solution)/shard_map/dot_general | solution.py:318
  195.2 7.8 %convolution_convert_fusion = bf16[512,1024]{1,0:T(8,128)(2,1)} fusion(bf16[1408,1024]{1,0:T(8,128)(2,1)S(1)} %copy-done, f32[512,1408]{1,0:T(8,128)} %fusion.9, bf16[2,1024,1408]{2,1,0:T(8,128)(2,1)} %param.20, bf16[512,1024]{1,0:T(8,128)(2,1)} %all-reduce.4.cloned.1.call-done, bf16[512,1024]{1,0:T(8,128)(2,1)} %param.15, f32[1024]{0:T(1024)S(1)} %copy-done.16, ...), kind=kOutput, calls=%fused_computation.32 | convolution fusion | flops 2963668992 | bytes 11802624 | tf_op jit(solution)/shard_map/dot_general | solution.py:321
  203.0 0.0 all-reduce.6.cloned.1.call-update
  203.1 0.2 all-reduce.8.cloned.1.call-start
  203.3 0.6 dynamic_slice.7.length
  203.9 0.1 select_reduce_fusion
  204.0 1.5 fusion.13
  205.5 2.4 fusion.22.q_ref
  207.9 35.4 %all-reduce.6.cloned.1.call-done = bf16[512,1024]{1,0:T(8,128)(2,1)} async-done(((bf16[512,1024]{1,0:T(8,128)(2,1)}), bf16[512,1024]{1,0:T(8,128)(2,1)}) %all-reduce.6.cloned.1.call-update) | async-done | bytes 1048592 | tf_op jit(solution)/shard_map/psum | solution.py:386
  243.4 2.6 multiply_reduce_fusion.1
  246.0 0.2 copy-done.9
  246.2 0.5 multiply_convert_fusion
  246.7 1.1 copy-done.13
  247.8 0.7 convolution_convert_fusion.2.v_ref
  248.5 0.2 copy-done.10
  248.7 0.7 convolution_convert_fusion.3.k_ref
  249.5 5.3 %cross_attend.1 = (bf16[8,128,512]{2,1,0:T(8,128)(2,1)S(1)}, f32[8,1,512]{2,1,0:T(1,128)S(1)}) custom-call(s32[1]{0:T(128)} %dynamic_slice.7.length, bf16[512,512]{1,0:T(8,128)(2,1)S(1)} %fusion.22.q_ref, bf16[512,512]{1,0:T(8,128)(2,1)S(1)} %convolution_convert_fusion.3.k_ref, bf16[512,512]{1,0:T(8,128)(2,1)S(1)} %convolution_convert_fusion.2.v_ref), custom_call_target="tpu_custom_call" | custom-call | tf_op jit(solution)/shard_map/cross_attend/pallas_call | solution.py:476
  254.8 1.0 copy-done.2
  255.8 0.1 reshape.141
  255.9 0.6 copy.54
  256.5 8.6 %exchange_3.1 = f32[16,8,32]{2,1,0:T(8,128)} custom-call(f32[16,8,32]{2,1,0:T(8,128)} %bitcast.85), custom_call_target="tpu_custom_call" | custom-call | tf_op jit(solution)/shard_map/exchange_3/pallas_call | solution.py:222
  265.1 0.9 reduce_max.9
  266.0 0.9 subtract_exponential_fusion
  266.8 3.8 mul.159
  270.6 7.3 %mul.160 = f32[16,64,512]{2,1,0:T(8,128)} reshape(f32[16,8,128,32]{3,2,1,0:T(8,128)} %mul.159) | data formatting | bytes 4194304 | tf_op jit(solution)/shard_map/mul | solution.py:419
  277.9 2.3 copy.43
  280.2 4.6 %copy.44 = bf16[16,8,128,32]{3,2,1,0:T(8,128)(2,1)} copy(bf16[16,8,128,32]{2,3,0,1:T(8,128)(2,1)} %bitcast.74) | data formatting | bytes 2097152 | tf_op jit(solution)/shard_map/transpose | solution.py:404
  284.8 6.8 %reshape.140.x_in = bf16[16,64,512]{2,1,0:T(8,128)(2,1)} reshape(bf16[16,8,128,32]{3,2,1,0:T(8,128)(2,1)} %copy.44) | data formatting | bytes 2097152 | tf_op jit(solution)/shard_map/reshape | solution.py:405
  291.6 24.2 %exchange_2.1 = bf16[16,64,512]{2,1,0:T(8,128)(2,1)} custom-call(bf16[16,64,512]{2,1,0:T(8,128)(2,1)} %reshape.140.x_in), custom_call_target="tpu_custom_call" | custom-call | tf_op jit(solution)/shard_map/exchange_2/pallas_call | solution.py:222
  315.7 2.2 multiply_reduce_fusion
  317.9 0.2 reduce_sum.62
  318.2 2.2 convolution_convert_fusion.8
  320.3 0.0 all-reduce.8.cloned.1.call-update
  320.4 0.0 all-gather.2.cloned.1.call-start
  320.4 26.2 %all-reduce.8.cloned.1.call-done = bf16[32,1024]{1,0:T(8,128)(2,1)} async-done(((bf16[32,1024]{1,0:T(8,128)(2,1)}), bf16[32,1024]{1,0:T(8,128)(2,1)}) %all-reduce.8.cloned.1.call-update) | async-done | bytes 65552 | tf_op jit(solution)/shard_map/psum | solution.py:425
  346.6 1.6 add_convert_fusion
  348.2 0.0 all-gather.2.cloned.1.call-update
  348.2 38.9 %all-gather.2.cloned.1.call-done = bf16[512,1024]{1,0:T(8,128)(2,1)} async-done(((bf16[32,1024]{1,0:T(8,128)(2,1)}), bf16[512,1024]{1,0:T(8,128)(2,1)}) %all-gather.2.cloned.1.call-update) | async-done | bytes 1048592 | tf_op jit(solution)/shard_map/all_gather | solution.py:441
  387.1 2.3 copy.59
  (40 shorter events, 0.2 us)
Async XLA Ops:
  7.2 188.0 %copy-start = (bf16[1408,1024]{1,0:T(8,128)(2,1)S(1)}, bf16[1408,1024]{1,0:T(8,128)(2,1)}, u32[]{:S(2)}) copy-start(bf16[1408,1024]{1,0:T(8,128)(2,1)} %param.21) | copy-start | bytes 8650756
  7.2 180.5 %all-reduce.4.cloned.1.call-start = ((), (), s32[]{:S(2)}) async-start(), calls=%async_computation | async-start | bytes 2097152 | tf_op jit(solution)/shard_map/psum | solution.py:381
  8.9 3.4 copy-start.4
  8.9 3.4 copy-start.12
  8.9 3.4 copy-start.15
  23.6 37.3 %copy-start.3 = (s32[16]{0:T(128)S(1)}, s32[16]{0:T(128)}, u32[]{:S(2)}) copy-start(s32[16]{0:T(128)} %lengths.1) | copy-start | bytes 196
  60.9 1.6 copy-start.1
  140.5 1.8 copy-start.14
  144.0 45.9 %copy-start.16 = (f32[1024]{0:T(1024)S(1)}, f32[1024]{0:T(1024)}, u32[]{:S(2)}) copy-start(f32[1024]{0:T(1024)} %param.19) | copy-start | bytes 12292
  144.0 99.4 %all-reduce.6.cloned.1.call-start = ((), (), s32[]{:S(2)}) async-start(), calls=%async_computation.1 | async-start | bytes 2097152 | tf_op jit(solution)/shard_map/psum | solution.py:386
  187.7 2.1 copy-start.5
  187.7 2.2 copy-start.7
  195.2 8.7 %copy-start.18 = (s32[4]{0:T(128)S(1)}, s32[4]{0:T(128)}, u32[]{:S(2)}) copy-start(s32[4]{0:T(128)} %param.25) | copy-start | bytes 52
  203.0 2.5 copy-start.17
  203.1 143.6 %all-reduce.8.cloned.1.call-start = ((), (), s32[]{:S(2)}) async-start(), calls=%async_computation.2 | async-start | bytes 131072 | tf_op jit(solution)/shard_map/psum | solution.py:425
  207.9 38.0 %copy-start.11 = (f32[1024]{0:T(1024)S(1)}, f32[1024]{0:T(1024)}, u32[]{:S(2)}) copy-start(f32[1024]{0:T(1024)} %param.22) | copy-start | bytes 12292
  243.4 2.6 copy-start.6
  243.4 2.6 copy-start.8
  243.4 2.8 copy-start.9
  246.2 1.6 copy-start.13
  247.8 1.0 copy-start.10
  254.8 1.0 copy-start.2
  320.4 66.8 %all-gather.2.cloned.1.call-start = ((), (), s32[]{:S(2)}) async-start(), calls=%async_computation.3 | async-start | bytes 1114112 | tf_op jit(solution)/shard_map/all_gather | solution.py:441
Sparse Core Ops, SparseCore 0:
  144.1 43.5 all-reduce.3
  203.2 40.1 all-reduce.5
  320.5 26.0 all-reduce.7
  349.2 37.8 all-gather.1

commit v2 on v1

--- a/solution.py
+++ b/solution.py
@@ -30,7 +30,9 @@
     return jnp.repeat(per_head.T, HD, axis=1)
 
 
-def greet_all(me, ring):
+def greet_all(ring, sides):
+    me = lax.axis_index("seq")
+    here = lax.axis_index("head")
     barrier = pltpu.get_barrier_semaphore()
 
     def greet(i, carry):
@@ -40,18 +42,39 @@
         return carry
 
     lax.fori_loop(1, ring, greet, 0)
-    pl.semaphore_wait(barrier, ring - 1)
-
-
-def scatter_kernel(ring, share, q_in, kv_in, q_out, kv_out, qs, qr, ks, kr, fs, fr, ls):
+    for k in range(1, sides):
+        pl.semaphore_signal(
+            barrier, inc=1, device_id={"head": lax.rem(here + k, sides)}, device_id_type=MESH
+        )
+    pl.semaphore_wait(barrier, ring - 1 + sides - 1)
+
+
+def side_copy(sides, k, source, target, send_sem, recv_sem):
+    here = lax.axis_index("head")
+    return pltpu.make_async_remote_copy(
+        src_ref=source,
+        dst_ref=target,
+        send_sem=send_sem,
+        recv_sem=recv_sem,
+        device_id={"head": lax.rem(here + k, sides)},
+        device_id_type=MESH,
+    )
+
+
+def scatter_kernel(
+    ring, share, sides, q_in, kv_in, w_in, q_out, kv_out, w_out, qs, qr, ks, kr, fs, fr, ls, ws, wr
+):
     me = lax.axis_index("seq")
+    here = lax.axis_index("head")
     part = kv_in.shape[1]
     mine = pl.ds(pl.multiple_of(lax.rem(me, share) * part, part), part)
     own_q = pltpu.make_async_copy(q_in.at[me], q_out.at[me], ls.at[0])
     own_kv = pltpu.make_async_copy(kv_in.at[me], kv_out.at[me, mine], ls.at[1])
     own_q.start()
     own_kv.start()
-    greet_all(me, ring)
+    own_w = pltpu.make_async_copy(w_in, w_out.at[here], ls.at[2])
+    own_w.start()
+    greet_all(ring, sides)
 
     def q_copy(i):
         to = lax.rem(me + i, ring)
@@ -111,6 +134,8 @@
         return carry
 
     lax.fori_loop(1, ring, send, 0)
+    for k in range(1, sides):
+        side_copy(sides, k, w_in, w_out.at[here], ws.at[k], wr.at[k]).start()
     own_kv.wait()
     for k in range(1, share):
         forward(0, k).start()
@@ -152,19 +177,24 @@
         return carry
 
     lax.fori_loop(0, ring, drain, 0)
+    for k in range(1, sides):
+        origin = lax.rem(here - k + sides, sides)
+        side_copy(sides, k, w_in, w_out.at[origin], ws.at[k], wr.at[k]).wait()
     own_q.wait()
-
-
-def scatter_heads(ring, share, q_send, kv_send):
+    own_w.wait()
+
+
+def scatter_heads(ring, share, sides, q_send, kv_send, weights):
     part = kv_send.shape[1]
     return pl.pallas_call(
-        functools.partial(scatter_kernel, ring, share),
+        functools.partial(scatter_kernel, ring, share, sides),
         out_shape=(
             jax.ShapeDtypeStruct(q_send.shape, q_send.dtype),
             jax.ShapeDtypeStruct((ring, part * share, 2 * HD), kv_send.dtype),
-        ),
-        in_specs=[pl.BlockSpec(memory_space=pltpu.VMEM)] * 2,
-        out_specs=(pl.BlockSpec(memory_space=pltpu.VMEM),) * 2,
+            jax.ShapeDtypeStruct((sides,) + weights.shape, weights.dtype),
+        ),
+        in_specs=[pl.BlockSpec(memory_space=pltpu.VMEM)] * 3,
+        out_specs=(pl.BlockSpec(memory_space=pltpu.VMEM),) * 3,
         scratch_shapes=[
             pltpu.SemaphoreType.DMA((ring,)),
             pltpu.SemaphoreType.DMA((ring,)),
@@ -172,66 +202,353 @@
             pltpu.SemaphoreType.DMA((ring,)),
             pltpu.SemaphoreType.DMA((ring, share)),
             pltpu.SemaphoreType.DMA((ring, share)),
-            pltpu.SemaphoreType.DMA((2,)),
+            pltpu.SemaphoreType.DMA((3,)),
+            pltpu.SemaphoreType.DMA((sides,)),
+            pltpu.SemaphoreType.DMA((sides,)),
         ],
-        compiler_params=pltpu.CompilerParams(collective_id=0, has_side_effects=True),
+        compiler_params=pltpu.CompilerParams(
+            collective_id=0, has_side_effects=True, vmem_limit_bytes=40 * 1024 * 1024
+        ),
         name="scatter_heads",
-    )(q_send, kv_send)
-
-
-def exchange_kernel(ring, x_in, x_out, ss, rs, ls):
+    )(q_send, kv_send, weights)
+
+
+def norm_rows(values, gain):
+    scale = lax.rsqrt(jnp.mean(values * values, axis=-1, keepdims=True) + epsilon)
+    return values * scale * gain
+
+
+def block_kernel(
+    ring, share, sides, x_in, w_out, tokens, g_ffn, g_final, up_hbm, down_hbm,
+    encoded,
+    context, hidden, normed, parts, up, down, ss, rs, fs, fr, ps, pr, ls,
+):
     me = lax.axis_index("seq")
-    own = pltpu.make_async_copy(x_in.at[me], x_out.at[me], ls)
+    here = lax.axis_index("head")
+    heads = ring // share
+    rows, width = tokens.shape
+    up_load = pltpu.make_async_copy(up_hbm, up, ls.at[0])
+    down_load = pltpu.make_async_copy(down_hbm, down, ls.at[1])
+    up_load.start()
+    down_load.start()
+
+    def place(side, origin):
+        return context.at[lax.rem(origin, share), side * heads + lax.div(origin, share)]
+
+    own = pltpu.make_async_copy(x_in.at[me], place(here, me), ls.at[2])
     own.start()
-    greet_all(me, ring)
+    greet_all(ring, sides)
 
     def outgoing(i):
         to = lax.rem(me + i, ring)
         return pltpu.make_async_remote_copy(
             src_ref=x_in.at[to],
-            dst_ref=x_out.at[me],
+            dst_ref=place(here, me),
             send_sem=ss.at[i],
             recv_sem=rs.at[i],
             device_id={"seq": to},
             device_id_type=MESH,
         )
 
+    def relay(i, k):
+        block = place(here, lax.rem(me - i + ring, ring))
+        return side_copy(sides, k, block, block, fs.at[i, k], fr.at[i, k])
+
     def send(i, carry):
         outgoing(i).start()
         return carry
 
     lax.fori_loop(1, ring, send, 0)
-
-    def finish(i, carry):
+    own.wait()
+    for k in range(1, sides):
+        relay(0, k).start()
+
+    def pass_on(i, carry):
         pltpu.make_async_remote_copy(
             src_ref=x_in.at[0],
-            dst_ref=x_out.at[lax.rem(me - i + ring, ring)],
+            dst_ref=place(here, lax.rem(me - i + ring, ring)),
             send_sem=ss.at[i],
             recv_sem=rs.at[i],
             device_id={"seq": lax.rem(me + i, ring)},
             device_id_type=MESH,
         ).wait_recv()
+        for k in range(1, sides):
+            relay(i, k).start()
+        return carry
+
+    lax.fori_loop(1, ring, pass_on, 0)
+
+    def sent(i, carry):
         outgoing(i).wait_send()
         return carry
 
-    lax.fori_loop(1, ring, finish, 0)
-    own.wait()
-
-
-def exchange(ring, blocks, which):
+    lax.fori_loop(1, ring, sent, 0)
+
+    def drain(i, carry):
+        for k in range(1, sides):
+            relay(i, k).wait_send()
+            origin = lax.rem(here - k + sides, sides)
+            block = place(origin, lax.rem(me - i + ring, ring))
+            side_copy(sides, k, block, block, fs.at[i, k], fr.at[i, k]).wait_recv()
+        return carry
+
+    lax.fori_loop(0, ring, drain, 0)
+    part = rows // share
+
+    def project(c, carry):
+        at = pl.ds(pl.multiple_of(c * part, part), part)
+        flat = context[c].reshape(sides * heads * HD, part)
+        total = tokens[at, :].astype(jnp.float32) + lax.dot_general(
+            flat, w_out[...], (((0,), (0,)), ((), ())), preferred_element_type=jnp.float32
+        )
+        hidden[at, :] = total
+        normed[at, :] = norm_rows(total, g_ffn[...]).astype(jnp.bfloat16)
+        return carry
+
+    lax.fori_loop(0, share, project, 0)
+    up_load.wait()
+    down_load.wait()
+    chunk = math.gcd(rows, 128)
+    chunks = rows // chunk
+
+    def span(c):
+        return pl.ds(pl.multiple_of(c * chunk, chunk), chunk)
+
+    def swap(c, k, side):
+        return side_copy(
+            sides, k, parts.at[side, span(c)], parts.at[side, span(c)], ps.at[c, k], pr.at[c, k]
+        )
+
+    def feed(c, carry):
+        x = normed[span(c), :]
+        gate = jnp.dot(x, up[0], preferred_element_type=jnp.float32)
+        lift = jnp.dot(x, up[1], preferred_element_type=jnp.float32)
+        active = (jax.nn.gelu(gate, approximate=True) * lift).astype(jnp.bfloat16)
+        parts[here, span(c), :] = jnp.dot(
+            active, down[...], preferred_element_type=jnp.float32
+        ).astype(jnp.bfloat16)
+        for k in range(1, sides):
+            swap(c, k, here).start()
+        return carry
+
+    lax.fori_loop(0, chunks, feed, 0)
+
+    def close(c, carry):
+        for k in range(1, sides):
+            swap(c, k, here).wait_send()
+            swap(c, k, lax.rem(here - k + sides, sides)).wait_recv()
+        total = hidden[span(c), :]
+        for side in range(sides):
+            total = total + parts[side, span(c), :].astype(jnp.float32)
+        encoded[span(c), :] = norm_rows(total, g_final[...]).astype(jnp.bfloat16)
+        return carry
+
+    lax.fori_loop(0, chunks, close, 0)
+
+
+def encoder_block(ring, share, sides, back, w_out, tokens, g_ffn, g_final, ffn_in, ffn_out):
+    rows, width = tokens.shape
+    chunks = rows // math.gcd(rows, 128)
+    vmem = pl.BlockSpec(memory_space=pltpu.VMEM)
+    hbm = pl.BlockSpec(memory_space=pl.ANY)
     return pl.pallas_call(
-        functools.partial(exchange_kernel, ring),
-        out_shape=jax.ShapeDtypeStruct(blocks.shape, blocks.dtype),
-        in_specs=[pl.BlockSpec(memory_space=pltpu.VMEM)],
-        out_specs=pl.BlockSpec(memory_space=pltpu.VMEM),
+        functools.partial(block_kernel, ring, share, sides),
+        out_shape=jax.ShapeDtypeStruct((rows, width), jnp.bfloat16),
+        in_specs=[vmem, vmem, vmem, vmem, vmem, hbm, hbm],
+        out_specs=vmem,
         scratch_shapes=[
+            pltpu.VMEM((share, sides * (ring // share), HD, rows // share), jnp.bfloat16),
+            pltpu.VMEM((rows, width), jnp.float32),
+            pltpu.VMEM((rows, width), jnp.bfloat16),
+            pltpu.VMEM((sides, rows, width), jnp.bfloat16),
+            pltpu.VMEM(ffn_in.shape, jnp.bfloat16),
+            pltpu.VMEM(ffn_out.shape, jnp.bfloat16),
             pltpu.SemaphoreType.DMA((ring,)),
             pltpu.SemaphoreType.DMA((ring,)),
-            pltpu.SemaphoreType.DMA,
+            pltpu.SemaphoreType.DMA((ring, sides)),
+            pltpu.SemaphoreType.DMA((ring, sides)),
+            pltpu.SemaphoreType.DMA((chunks, sides)),
+            pltpu.SemaphoreType.DMA((chunks, sides)),
+            pltpu.SemaphoreType.DMA((3,)),
         ],
-        compiler_params=pltpu.CompilerParams(collective_id=which, has_side_effects=True),
-        name=f"exchange_{which}",
-    )(blocks)
+        compiler_params=pltpu.CompilerParams(
+            collective_id=1, has_side_effects=True, vmem_limit_bytes=50 * 1024 * 1024
+        ),
+        name="encoder_block",
+    )(back, w_out, tokens, g_ffn[None, :], g_final[None, :], ffn_in, ffn_out)
+
+
+def merge_kernel(
+    ring, sides, mixed, stats, w_ref, mine, live, decoded,
+    got, got_stats, parts, ms, mr, ts, tr, ps, pr, ds, dr, fs, fr, ls,
+):
+    me = lax.axis_index("seq")
+    here = lax.axis_index("head")
+    rows, width = mine.shape
+    mate = me + 1 - 2 * lax.rem(me, 2)
+
+    def slab(owner):
+        return pl.ds(pl.multiple_of(owner * rows, rows), rows)
+
+    own_mixed = pltpu.make_async_copy(mixed.at[slab(me)], got.at[me], ls.at[0])
+    own_stats = pltpu.make_async_copy(stats.at[slab(me)], got_stats.at[me], ls.at[1])
+    own_mixed.start()
+    own_stats.start()
+    greet_all(ring, sides)
+
+    def copies(i, origin):
+        to = lax.rem(me + i, ring)
+        return (
+            pltpu.make_async_remote_copy(
+                src_ref=mixed.at[slab(to)],
+                dst_ref=got.at[origin],
+                send_sem=ms.at[i],
+                recv_sem=mr.at[i],
+                device_id={"seq": to},
+                device_id_type=MESH,
+            ),
+            pltpu.make_async_remote_copy(
+                src_ref=stats.at[slab(to)],
+                dst_ref=got_stats.at[origin],
+                send_sem=ts.at[i],
+                recv_sem=tr.at[i],
+                device_id={"seq": to},
+                device_id_type=MESH,
+            ),
+        )
+
+    def send(i, carry):
+        for copy in copies(i, me):
+            copy.start()
+        return carry
+
+    lax.fori_loop(1, ring, send, 0)
+
+    def collect(i, carry):
+        for copy in copies(i, lax.rem(me - i + ring, ring)):
+            copy.wait()
+        return carry
+
+    lax.fori_loop(1, ring, collect, 0)
+    own_mixed.wait()
+    own_stats.wait()
+    heads = w_ref.shape[0] // HD
+    seen = got_stats[...]
+    best = jnp.max(seen, axis=0, keepdims=True)
+    grow = jnp.exp(seen - best)
+    sums = pltpu.roll(seen.reshape(ring * rows, 2 * HD), HD, 1).reshape(ring, rows, 2 * HD)
+    weight_sum = jnp.sum(grow * sums, axis=0, keepdims=True)
+    factor = (grow / weight_sum).reshape(ring * rows, 2 * HD)
+    lane = lax.broadcasted_iota(jnp.int32, (2 * HD, heads * HD), 1)
+    row = lax.broadcasted_iota(jnp.int32, (2 * HD, heads * HD), 0)
+    spread = jnp.where((lane >= row * HD) & (lane < row * HD + HD), 1.0, 0.0)
+    factor = jnp.where(
+        lax.broadcasted_iota(jnp.int32, factor.shape, 1) < heads, factor, 0.0
+    )
+    wide = jnp.dot(
+        factor, spread, precision=lax.Precision.HIGHEST, preferred_element_type=jnp.float32
+    ).reshape(ring, rows, heads * HD)
+    context = jnp.sum(got[...].astype(jnp.float32) * wide, axis=0).astype(jnp.bfloat16)
+    parts[here] = jnp.dot(context, w_ref[...], preferred_element_type=jnp.float32).astype(
+        jnp.bfloat16
+    )
+
+    def swap(k, side):
+        return side_copy(sides, k, parts.at[side], parts.at[side], ps.at[k], pr.at[k])
+
+    for k in range(1, sides):
+        swap(k, here).start()
+    for k in range(1, sides):
+        swap(k, here).wait_send()
+        swap(k, lax.rem(here - k + sides, sides)).wait_recv()
+    total = parts[0].astype(jnp.float32)
+    for side in range(1, sides):
+        total = total + parts[side].astype(jnp.float32)
+    decoded[slab(me), :] = (
+        mine[...].astype(jnp.float32) + jnp.where(live[...] > 0.0, total, 0.0)
+    ).astype(jnp.bfloat16)
+
+    def spread_out(j, owner):
+        block = decoded.at[slab(owner)]
+        return pltpu.make_async_remote_copy(
+            src_ref=block,
+            dst_ref=block,
+            send_sem=ds.at[j],
+            recv_sem=dr.at[j],
+            device_id={"seq": lax.rem(me + 2 * j, ring)},
+            device_id_type=MESH,
+        )
+
+    def hand_over(j, owner):
+        block = decoded.at[slab(owner)]
+        return pltpu.make_async_remote_copy(
+            src_ref=block,
+            dst_ref=block,
+            send_sem=fs.at[j],
+            recv_sem=fr.at[j],
+            device_id={"seq": mate},
+            device_id_type=MESH,
+        )
+
+    def share_out(j, carry):
+        spread_out(j, me).start()
+        return carry
+
+    lax.fori_loop(1, ring // 2, share_out, 0)
+    hand_over(0, me).start()
+
+    def pass_on(j, carry):
+        owner = lax.rem(me - 2 * j + ring, ring)
+        spread_out(j, owner).wait_recv()
+        hand_over(j, owner).start()
+        return carry
+
+    lax.fori_loop(1, ring // 2, pass_on, 0)
+
+    def finish(j, carry):
+        spread_out(j, me).wait_send()
+        return carry
+
+    lax.fori_loop(1, ring // 2, finish, 0)
+
+    def drain(j, carry):
+        hand_over(j, lax.rem(me - 2 * j + ring, ring)).wait_send()
+        hand_over(j, lax.rem(mate - 2 * j + ring, ring)).wait_recv()
+        return carry
+
+    lax.fori_loop(0, ring // 2, drain, 0)
+
+
+def merge_targets(ring, sides, mixed, stats, weights, mine, live):
+    rows, width = mine.shape
+    vmem = pl.BlockSpec(memory_space=pltpu.VMEM)
+    dma = pltpu.SemaphoreType.DMA
+    return pl.pallas_call(
+        functools.partial(merge_kernel, ring, sides),
+        out_shape=jax.ShapeDtypeStruct((rows * ring, width), jnp.bfloat16),
+        in_specs=[vmem] * 5,
+        out_specs=vmem,
+        scratch_shapes=[
+            pltpu.VMEM((ring, rows, mixed.shape[1]), jnp.bfloat16),
+            pltpu.VMEM((ring, rows, stats.shape[1]), jnp.float32),
+            pltpu.VMEM((sides, rows, width), jnp.bfloat16),
+            dma((ring,)),
+            dma((ring,)),
+            dma((ring,)),
+            dma((ring,)),
+            dma((sides,)),
+            dma((sides,)),
+            dma((ring,)),
+            dma((ring,)),
+            dma((ring,)),
+            dma((ring,)),
+            dma((2,)),
+        ],
+        compiler_params=pltpu.CompilerParams(
+            collective_id=2, has_side_effects=True, vmem_limit_bytes=40 * 1024 * 1024
+        ),
+        name="merge_targets",
+    )(mixed, stats, weights, mine, live)
 
 
 def attend_kernel(lengths, q_ref, kv_ref, o_ref, keys, values, count):
@@ -314,15 +631,9 @@
     )(pad_lengths, q_all, kv_all)
 
 
-def feed_forward(normed_in, ffn_in, ffn_out):
-    gate_proj = jnp.dot(normed_in, ffn_in[0], preferred_element_type=jnp.float32)
-    up_proj = jnp.dot(normed_in, ffn_in[1], preferred_element_type=jnp.float32)
-    activated = (jax.nn.gelu(gate_proj, approximate=True) * up_proj).astype(jnp.bfloat16)
-    return jnp.dot(activated, ffn_out, preferred_element_type=jnp.float32)
-
-
 def local(
     ring,
+    sides,
     tokens,
     norm_attn,
     self_qkv,
@@ -365,31 +676,27 @@
         axis=2,
     )
     kv_send = kv_local.transpose(1, 0, 2).reshape(ring, part, 2 * HD)
-    q_got, kv_got = scatter_heads(ring, share, q_send, kv_send)
+    q_got, kv_got, out_all = scatter_heads(ring, share, sides, q_send, kv_send, self_out)
     q_all = q_got.transpose(1, 0, 2).reshape(HD, ring * part)
     mixed_t = attend(q_all, kv_got, pad_lengths)
     back = mixed_t.reshape(HD, ring, part).transpose(1, 0, 2)
-    context_t = (
-        exchange(ring, back, 1)
-        .reshape(heads_here, share, HD, part)
-        .transpose(0, 2, 1, 3)
-        .reshape(heads_here * HD, row_count)
-    )
-    attn_part = lax.dot_general(
-        context_t, self_out, (((0,), (0,)), ((), ())), preferred_element_type=jnp.float32
-    )
-    hidden_in = tokens.astype(jnp.float32) + lax.psum(
-        attn_part.astype(jnp.bfloat16), "head"
-    ).astype(jnp.float32)
-    ffn_normed = rms_norm(hidden_in, norm_ffn).astype(jnp.bfloat16)
-    ffn_part = feed_forward(ffn_normed, ffn_in, ffn_out)
-    final_in = hidden_in + lax.psum(ffn_part.astype(jnp.bfloat16), "head").astype(jnp.float32)
-    encoded = rms_norm(final_in, norm_final).astype(jnp.bfloat16)
+    encoded = encoder_block(
+        ring,
+        share,
+        sides,
+        back,
+        out_all.reshape(-1, out_all.shape[2]),
+        tokens,
+        norm_ffn,
+        norm_final,
+        ffn_in,
+        ffn_out,
+    )
     target_rows = targets.shape[0]
     cross_normed = rms_norm(targets, norm_cross).astype(jnp.bfloat16)
-    cross_q_t = lax.dot_general(
-        cross_query, cross_normed, (((0,), (1,)), ((), ())), preferred_element_type=jnp.float32
-    ).astype(jnp.bfloat16) * jnp.bfloat16(scaling)
+    cross_q = jnp.dot(cross_normed, cross_query, preferred_element_type=jnp.float32).astype(
+        jnp.bfloat16
+    ) * jnp.bfloat16(scaling)
     cross_keys = jnp.dot(encoded, cross_kv[0], preferred_element_type=jnp.float32).astype(
         jnp.bfloat16
     )
@@ -397,32 +704,8 @@
         jnp.bfloat16
     )
     my_length = lax.dynamic_slice_in_dim(pad_lengths, lax.axis_index("seq"), 1, 0)
-    mixed, top = cross_attend(my_length, cross_q_t, cross_keys, cross_values)
+    mixed, stats = cross_attend(my_length, cross_q, cross_keys, cross_values)
     slice_rows = target_rows // ring
-    sent = (
-        mixed.reshape(heads_here, 2 * HD, ring, slice_rows)
-        .transpose(2, 0, 1, 3)
-        .reshape(ring, heads_here * 2 * HD * slice_rows // 512, 512)
-    )
-    got = exchange(ring, sent, 2).reshape(ring, heads_here, 2 * HD, slice_rows)
-    tops = exchange(
-        ring,
-        jnp.broadcast_to(
-            top.reshape(heads_here, 1, ring, slice_rows)
-            .transpose(2, 0, 1, 3)
-            .reshape(ring, heads_here, slice_rows),
-            (ring, heads_here, slice_rows),
-        ),
-        3,
-    ).reshape(ring, heads_here, 1, slice_rows)
-    best = jnp.max(tops, axis=0, keepdims=True)
-    summed = jnp.sum(got.astype(jnp.float32) * jnp.exp(tops - best), axis=0)
-    cross_context = (summed[:, HD:, :] / summed[:, 0:1, :]).astype(jnp.bfloat16)
-    cross_context = cross_context.reshape(heads_here * HD, slice_rows)
-    cross_part = lax.dot_general(
-        cross_context, cross_out, (((0,), (0,)), ((), ())), preferred_element_type=jnp.float32
-    )
-    cross_total = lax.psum(cross_part.astype(jnp.bfloat16), "head").astype(jnp.float32)
     slots = lax.axis_index("seq") * slice_rows + jnp.arange(slice_rows, dtype=jnp.int32)
     owner = slots // TGT_LEN
     limits = jnp.sum(
@@ -435,70 +718,78 @@
     )
     target_live = slots % TGT_LEN < limits
     mine = lax.dynamic_slice_in_dim(targets, lax.axis_index("seq") * slice_rows, slice_rows, 0)
-    decoded_here = (
-        mine.astype(jnp.float32) + jnp.where(target_live[:, None], cross_total, 0.0)
-    ).astype(jnp.bfloat16)
-    decoded = lax.all_gather(decoded_here, "seq", axis=0, tiled=True)
+    live = jnp.broadcast_to(target_live[:, None], mine.shape).astype(jnp.float32)
+    decoded = merge_targets(ring, sides, mixed, stats, cross_out, mine, live)
     return (encoded, decoded)
 
 
-def cross_kernel(length, q_ref, k_ref, v_ref, o_ref, top_ref):
+def cross_kernel(length, q_ref, k_ref, v_ref, o_ref, stats):
+    i = pl.program_id(0)
     rows = k_ref.shape[0]
-    queries = q_ref.shape[1]
-    live = lax.broadcasted_iota(jnp.int32, (rows, queries), 0) < length[0]
+    queries = q_ref.shape[0]
+    live = lax.broadcasted_iota(jnp.int32, (queries, rows), 1) < length[0]
     lane = lax.broadcasted_iota(jnp.int32, (rows, 2 * HD), 1)
+    out_lane = lax.broadcasted_iota(jnp.int32, (queries, 2 * HD), 1)
     ones = jnp.ones((rows, 2 * HD), jnp.bfloat16)
+
+    @pl.when(i == 0)
+    def clear():
+        stats[...] = jnp.where(out_lane < HD, 0.0, 1.0)
+
+    pieces = []
     for h in range(2):
         own = lane < HD if h == 0 else lane >= HD
         keys = jnp.where(own, k_ref[...], jnp.zeros_like(ones))
         values = jnp.where(own, v_ref[...], ones)
         scores = lax.dot_general(
-            keys, q_ref[...], (((1,), (0,)), ((), ())), preferred_element_type=jnp.float32
+            q_ref[...], keys, (((1,), (1,)), ((), ())), preferred_element_type=jnp.float32
         )
         scores = jnp.where(live, scores, masked_score)
-        top = jnp.max(scores, axis=0, keepdims=True)
+        top = jnp.max(scores, axis=1, keepdims=True)
         weights = jnp.exp(scores - top).astype(jnp.bfloat16)
-        part = lax.dot_general(
-            values, weights, (((0,), (0,)), ((), ())), preferred_element_type=jnp.float32
-        ).astype(jnp.bfloat16)
-        if h == 0:
-            o_ref[0, :HD, :] = part[HD:, :]
-            o_ref[0, HD:, :] = part[:HD, :]
-        else:
-            o_ref[1] = part
-        top_ref[h] = top
-
-
-def cross_attend(my_length, q_t, keys, values):
+        part = jnp.dot(weights, values, preferred_element_type=jnp.float32)
+        total = part[:, 2 * HD - 1 :] if h == 0 else part[:, :1]
+        stats[...] = jnp.where(
+            out_lane == 2 * i + h,
+            top,
+            jnp.where(out_lane == HD + 2 * i + h, total, stats[...]),
+        )
+        pieces.append(part)
+    o_ref[...] = jnp.where(out_lane < HD, pieces[0], pieces[1]).astype(jnp.bfloat16)
+
+
+def cross_attend(my_length, q_all, keys, values):
     rows, width = keys.shape
-    queries = q_t.shape[1]
-    heads = width // HD
+    queries = q_all.shape[0]
     return pl.pallas_call(
         cross_kernel,
         out_shape=(
-            jax.ShapeDtypeStruct((heads, 2 * HD, queries), jnp.bfloat16),
-            jax.ShapeDtypeStruct((heads, 1, queries), jnp.float32),
+            jax.ShapeDtypeStruct((queries, width), jnp.bfloat16),
+            jax.ShapeDtypeStruct((queries, 2 * HD), jnp.float32),
         ),
         grid_spec=pltpu.PrefetchScalarGridSpec(
             num_scalar_prefetch=1,
-            grid=(heads // 2,),
+            grid=(width // (2 * HD),),
             in_specs=[
-                pl.BlockSpec((2 * HD, queries), lambda i, n: (i, 0)),
+                pl.BlockSpec((queries, 2 * HD), lambda i, n: (0, i)),
                 pl.BlockSpec((rows, 2 * HD), lambda i, n: (0, i)),
                 pl.BlockSpec((rows, 2 * HD), lambda i, n: (0, i)),
             ],
             out_specs=(
-                pl.BlockSpec((2, 2 * HD, queries), lambda i, n: (i, 0, 0)),
-                pl.BlockSpec((2, 1, queries), lambda i, n: (i, 0, 0)),
+                pl.BlockSpec((queries, 2 * HD), lambda i, n: (0, i)),
+                pl.BlockSpec((queries, 2 * HD), lambda i, n: (0, 0)),
             ),
         ),
-        compiler_params=pltpu.CompilerParams(vmem_limit_bytes=32 * 1024 * 1024),
+        compiler_params=pltpu.CompilerParams(
+            dimension_semantics=("arbitrary",), vmem_limit_bytes=32 * 1024 * 1024
+        ),
         name="cross_attend",
-    )(my_length, q_t, keys, values)
+    )(my_length, q_all, keys, values)
 
 
 def solution(mesh):
     ring = mesh.shape["seq"]
+    sides = mesh.shape["head"]
     placed = (
         P("seq", None),
         P(),
@@ -517,7 +808,7 @@
         P("head", None),
     )
     return jax.shard_map(
-        functools.partial(local, ring),
+        functools.partial(local, ring, sides),
         mesh=mesh,
         in_specs=placed,
         out_specs=(P("seq", None), P()),

time: 397 us -> 227 us (0.57)
  waiting for transfers between devices: 144 us -> 0 us
  Pallas kernels: 151 us -> 192 us
  local copies, waits for them, and re-layouts: 42 us -> 15.6 us
  matrix products: 26.7 us -> 10.7 us
  between operations: 14.1 us -> 0.91 us
  other arithmetic: 17.2 us -> 5.34 us
    psum x3 -> x0, waiting for transfers between devices: 105 us -> none  [the longest x1 43.7 us: local(): lax.psum(attn_part.astype(jnp.bfloat16), 'head').astype(jnp.float32)]
    pallas_call x5 -> x4, Pallas kernels: 98.6 us -> 139 us  [the longest x1 61.2 us: encoder_block(): pl.pallas_call(functools.partial(block_kernel, ring, share, sides), out_s...]
    all_gather x1 -> x0, waiting for transfers between devices: 38.9 us -> none  [local(): decoded = lax.all_gather(decoded_here, 'seq', axis=0, tiled=True)]
    dot_general x5 -> x1, matrix products: 19.4 us -> 1.99 us  [local(): jnp.dot(cross_normed, cross_query, preferred_element_type=jnp.float32)]
    reshape x4 -> x0, local copies, waits for them, and re-layouts: 9.17 us -> none  [the longest x1 6.78 us: local(): sent = mixed.reshape(heads_here, 2 * HD, ring, slice_rows).transpose(2, 0...]
    mul x2 -> x1, local copies, waits for them, and re-layouts: 11.1 us -> 2.05 us  [local(): lax.dot_general(self_qkv[0], normed, (((0,), (1,)), ((), ())), preferred_...]
    reduce_sum x4 -> x2, other arithmetic: 7.81 us -> 3.09 us  [rms_norm(): jnp.mean(widened * widened, axis=-1, keepdims=True) + epsilon]
    transpose x1 -> x0, local copies, waits for them, and re-layouts: 4.58 us -> none  [local(): sent = mixed.reshape(heads_here, 2 * HD, ring, slice_rows).transpose(2, 0...]
  transfers between devices with their start and end apart: 4 -> 0, of which waited for: 4 -> 0; matrix products, arithmetic and copies ran while one was open for 1% -> 0% of each run, Pallas kernels for 0% -> 0%
where the time goes in v2:
time: 227 us; the launch traced here: 224 us
  Pallas kernels  192 us (85%)
  local copies, waits for them, and re-layouts  15.6 us (7%)
  matrix products  10.7 us (5%)
  other arithmetic  5.34 us (2%)
    pallas_call x1, Pallas kernels, encoder_block(): pl.pallas_call(functools.partial(block_kernel, ring, share, sides), out_s...  61.2 us
    pallas_call x1, Pallas kernels, attend(): pl.pallas_call(attend_kernel, out_shape=jax.ShapeDtypeStruct((HD, total),...  52.8 us
    pallas_call x1, Pallas kernels, merge_targets(): pl.pallas_call(functools.partial(merge_kernel, ring, sides), out_shape=ja...  38.5 us
    pallas_call x1, Pallas kernels, scatter_heads(): pl.pallas_call(functools.partial(scatter_kernel, ring, share, sides), out...  33.4 us
    unnamed x30, local copies, waits for them, and re-layouts  6.28 us
    pallas_call x1, Pallas kernels, cross_attend(): pl.pallas_call(cross_kernel, out_shape=(jax.ShapeDtypeStruct((queries, wi...  5.58 us

profile of v2, /device:TPU:0, one launch (start us, length us, event | category | flops | bytes accessed | tf_op | source)
XLA Modules:
  0.0 224.1 jit_solution(15681289629232741594)
XLA Ops:
  0.6 0.0 copy-start
  0.6 1.6 fusion
  2.2 0.0 copy-start.1
  2.3 0.0 copy-start.11
  2.3 2.5 %convolution_convert_fusion.4 = bf16[512,512]{0,1:T(8,128)(2,1)S(1)} fusion(bf16[3,1024,512]{2,1,0:T(8,128)(2,1)} %param.17, bf16[512,1024]{1,0:T(8,128)(2,1)} %tokens.1, f32[1024]{0:T(1024)} %param.16, f32[512]{0:T(512)S(1)} %add_rsqrt_fusion.1), kind=kOutput, calls=%fused_computation.14 | convolution fusion | flops 539230208 | bytes 2627584 | tf_op jit(solution)/shard_map/dot_general | solution.py:662
  4.8 1.3 copy.29
  6.1 0.0 copy-done.1
  6.1 0.0 copy-done.11
  6.1 2.1 convolution_convert_fusion.3
  8.2 1.3 copy.30
  9.5 2.1 pad_maximum_fusion
  11.6 2.8 %fusion.7 = bf16[512,512]{0,1:T(8,128)(2,1)} fusion(bf16[3,1024,512]{2,1,0:T(8,128)(2,1)} %param.17, bf16[512,1024]{1,0:T(8,128)(2,1)S(1)} %copy-done.1, f32[1024]{0:T(1024)S(1)} %copy-done.11, f32[512]{0:T(512)S(1)} %add_rsqrt_fusion.1), kind=kOutput, calls=%fused_computation.17 | convolution fusion | flops 539492352 | bytes 2627584 | tf_op jit(solution)/shard_map/dot_general | solution.py:659
  14.4 2.0 copy.27
  16.4 2.0 reshape.82
  18.4 1.1 copy.28
  19.5 0.0 copy-start.9
  19.5 0.0 copy-start.4
  19.5 1.2 copy-done.4
  20.8 33.4 %scatter_heads.1 = (bf16[16,64,256]{2,1,0:T(8,128)(2,1)S(1)}, bf16[16,512,128]{2,1,0:T(8,128)(2,1)S(1)}, bf16[2,512,1024]{2,1,0:T(8,128)(2,1)S(1)}) custom-call(bf16[16,64,256]{2,1,0:T(8,128)(2,1)S(1)} %bitcast.41, bf16[16,256,128]{2,1,0:T(8,128)(2,1)S(1)} %bitcast.40, bf16[512,1024]{1,0:T(8,128)(2,1)S(1)} %copy-done.4), custom_call_target="tpu_custom_call" | custom-call | tf_op jit(solution)/shard_map/scatter_heads/pallas_call | solution.py:189
  54.2 0.0 copy-start.2
  54.2 0.0 copy-done.9
  54.2 0.0 copy-start.7
  54.2 0.0 copy-start.8
  54.3 52.8 %attend.1 = bf16[64,4096]{1,0:T(8,128)(2,1)S(1)} custom-call(s32[16]{0:T(128)S(1)} %copy-done.9, bf16[64,4096]{1,0:T(8,128)(2,1)S(1)} %bitcast.43, bf16[16,512,128]{2,1,0:T(8,128)(2,1)S(1)} %get-tuple-element.8.kv_ref), custom_call_target="tpu_custom_call" | custom-call | tf_op jit(solution)/shard_map/attend/pallas_call | solution.py:610
  107.1 0.0 copy-done.2
  107.2 0.0 copy-done.7
  107.2 0.0 copy-done.8
  107.2 0.0 copy-start.10
  107.2 61.2 %encoder_block.1 = bf16[512,1024]{1,0:T(8,128)(2,1)S(1)} custom-call(bf16[16,64,256]{2,1,0:T(8,128)(2,1)S(1)} %bitcast.42, bf16[1024,1024]{1,0:T(8,128)(2,1)} %bitcast.45, bf16[512,1024]{1,0:T(8,128)(2,1)S(1)} %copy-done.1, f32[1,1024]{1,0:T(1,128)S(1)} %bitcast.47, f32[1,1024]{1,0:T(1,128)S(1)} %bitcast.48, bf16[2,1024,1408]{2,1,0:T(8,128)(2,1)} %up_hbm.1, ...), custom_call_target="tpu_custom_call" | custom-call | tf_op jit(solution)/shard_map/encoder_block/pallas_call | solution.py:354
  168.4 0.0 copy-done.10
  168.4 0.7 convolution_convert_fusion.v_ref
  169.1 0.0 copy-start.12
  169.2 0.7 convolution_convert_fusion.1.k_ref
  169.9 0.6 dynamic_slice.6.length
  170.5 1.5 fusion.3
  172.0 0.0 copy-done
  172.0 0.0 copy-done.12
  172.0 0.0 copy-start.13
  172.0 2.0 fusion.8.q_ref
  174.0 5.6 %cross_attend.1 = (bf16[512,512]{1,0:T(8,128)(2,1)S(1)}, f32[512,128]{1,0:T(8,128)S(1)}) custom-call(s32[1]{0:T(128)} %dynamic_slice.6.length, bf16[512,512]{1,0:T(8,128)(2,1)S(1)} %fusion.8.q_ref, bf16[512,512]{1,0:T(8,128)(2,1)S(1)} %convolution_convert_fusion.1.k_ref, bf16[512,512]{1,0:T(8,128)(2,1)S(1)} %convolution_convert_fusion.v_ref), custom_call_target="tpu_custom_call" | custom-call | tf_op jit(solution)/shard_map/cross_attend/pallas_call | solution.py:764
  179.6 0.0 copy-start.5
  179.6 0.8 copy-done.5
  180.4 0.8 constant_dynamic-slice_fusion.mine
  181.2 0.0 copy-done.13
  181.3 0.1 select_reduce_fusion
  181.4 0.1 broadcast_in_dim.35.live
  181.4 0.0 copy-start.3
  181.4 1.2 copy-done.3
  182.7 0.0 copy-start.6
  182.7 1.0 copy-done.6
  183.7 38.5 %merge_targets.1 = bf16[512,1024]{1,0:T(8,128)(2,1)S(1)} custom-call(bf16[512,512]{1,0:T(8,128)(2,1)S(1)} %copy-done.6, f32[512,128]{1,0:T(8,128)S(1)} %get-tuple-element.11.stats, bf16[512,1024]{1,0:T(8,128)(2,1)S(1)} %copy-done.3, bf16[32,1024]{1,0:T(8,128)(2,1)S(1)} %constant_dynamic-slice_fusion.mine, f32[32,1024]{1,0:T(8,128)S(1)} %broadcast_in_dim.35.live), custom_call_target="tpu_custom_call" | custom-call | tf_op jit(solution)/shard_map/merge_targets/pallas_call | solution.py:526
  222.2 1.0 copy.39
  223.2 1.0 copy.40
  (6 shorter events, 0.1 us)
Async XLA Ops:
  0.6 171.4 %copy-start = (bf16[1024,512]{1,0:T(8,128)(2,1)S(1)}, bf16[1024,512]{1,0:T(8,128)(2,1)}, u32[]{:S(2)}) copy-start(bf16[1024,512]{1,0:T(8,128)(2,1)} %param.27) | copy-start | bytes 3145732
  2.2 3.8 %copy-start.1 = (bf16[512,1024]{1,0:T(8,128)(2,1)S(1)}, bf16[512,1024]{1,0:T(8,128)(2,1)}, u32[]{:S(2)}) copy-start(bf16[512,1024]{1,0:T(8,128)(2,1)} %tokens.1) | copy-start | bytes 3145732
  2.3 3.8 %copy-start.11 = (f32[1024]{0:T(1024)S(1)}, f32[1024]{0:T(1024)}, u32[]{:S(2)}) copy-start(f32[1024]{0:T(1024)} %param.16) | copy-start | bytes 12292
  19.5 34.7 %copy-start.9 = (s32[16]{0:T(128)S(1)}, s32[16]{0:T(128)}, u32[]{:S(2)}) copy-start(s32[16]{0:T(128)} %lengths.1) | copy-start | bytes 196
  19.5 1.2 copy-start.4
  54.2 52.9 %copy-start.2 = (bf16[2,512,1024]{2,1,0:T(8,128)(2,1)}, bf16[2,512,1024]{2,1,0:T(8,128)(2,1)S(1)}, u32[]{:S(2)}) copy-start(bf16[2,512,1024]{2,1,0:T(8,128)(2,1)S(1)} %get-tuple-element.9) | copy-start | bytes 6291460
  54.2 52.9 %copy-start.7 = (f32[1024]{0:T(1024)S(1)}, f32[1024]{0:T(1024)}, u32[]{:S(2)}) copy-start(f32[1024]{0:T(1024)} %param.19) | copy-start | bytes 12292
  54.2 52.9 %copy-start.8 = (f32[1024]{0:T(1024)S(1)}, f32[1024]{0:T(1024)}, u32[]{:S(2)}) copy-start(f32[1024]{0:T(1024)} %param.22) | copy-start | bytes 12292
  107.2 61.2 %copy-start.10 = (bf16[2,1024,512]{2,1,0:T(8,128)(2,1)S(1)}, bf16[2,1024,512]{2,1,0:T(8,128)(2,1)}, u32[]{:S(2)}) copy-start(bf16[2,1024,512]{2,1,0:T(8,128)(2,1)} %param.28) | copy-start | bytes 6291460
  169.1 2.8 %copy-start.12 = (f32[1024]{0:T(1024)S(1)}, f32[1024]{0:T(1024)}, u32[]{:S(2)}) copy-start(f32[1024]{0:T(1024)} %param.26) | copy-start | bytes 12292
  172.0 9.2 %copy-start.13 = (s32[4]{0:T(128)S(1)}, s32[4]{0:T(128)}, u32[]{:S(2)}) copy-start(s32[4]{0:T(128)} %param.25) | copy-start | bytes 52
  179.6 0.8 copy-start.5
  181.4 1.2 copy-start.3
  182.7 1.0 copy-start.6

commit v3 on v2

--- a/solution.py
+++ b/solution.py
@@ -15,19 +15,6 @@
 epsilon = 1e-06
 masked_score = -1e30
 MESH = pl.DeviceIdType.MESH
-
-
-def rms_norm(values, gain_vector):
-    widened = values.astype(jnp.float32)
-    return (
-        widened
-        * lax.rsqrt(jnp.mean(widened * widened, axis=-1, keepdims=True) + epsilon)
-        * gain_vector
-    )
-
-
-def spread_heads(per_head):
-    return jnp.repeat(per_head.T, HD, axis=1)
 
 
 def greet_all(ring, sides):
@@ -62,7 +49,8 @@
 
 
 def scatter_kernel(
-    ring, share, sides, q_in, kv_in, w_in, q_out, kv_out, w_out, qs, qr, ks, kr, fs, fr, ls, ws, wr
+    ring, share, sides, q_in, kv_in, w_in, targets, g_cross, w_cross,
+    q_out, kv_out, w_out, cross_q, qs, qr, ks, kr, fs, fr, ls, ws, wr,
 ):
     me = lax.axis_index("seq")
     here = lax.axis_index("head")
@@ -137,6 +125,10 @@
     for k in range(1, sides):
         side_copy(sides, k, w_in, w_out.at[here], ws.at[k], wr.at[k]).start()
     own_kv.wait()
+    cross_normed = norm_rows(targets[...].astype(jnp.float32), g_cross[...]).astype(jnp.bfloat16)
+    cross_q[...] = jnp.dot(
+        cross_normed, w_cross[...], preferred_element_type=jnp.float32
+    ).astype(jnp.bfloat16) * jnp.bfloat16(HD ** (-0.5))
     for k in range(1, share):
         forward(0, k).start()
 
@@ -184,7 +176,7 @@
     own_w.wait()
 
 
-def scatter_heads(ring, share, sides, q_send, kv_send, weights):
+def scatter_heads(ring, share, sides, q_send, kv_send, weights, targets, g_cross, w_cross):
     part = kv_send.shape[1]
     return pl.pallas_call(
         functools.partial(scatter_kernel, ring, share, sides),
@@ -192,9 +184,10 @@
             jax.ShapeDtypeStruct(q_send.shape, q_send.dtype),
             jax.ShapeDtypeStruct((ring, part * share, 2 * HD), kv_send.dtype),
             jax.ShapeDtypeStruct((sides,) + weights.shape, weights.dtype),
-        ),
-        in_specs=[pl.BlockSpec(memory_space=pltpu.VMEM)] * 3,
-        out_specs=(pl.BlockSpec(memory_space=pltpu.VMEM),) * 3,
+            jax.ShapeDtypeStruct((targets.shape[0], w_cross.shape[1]), jnp.bfloat16),
+        ),
+        in_specs=[pl.BlockSpec(memory_space=pltpu.VMEM)] * 6,
+        out_specs=(pl.BlockSpec(memory_space=pltpu.VMEM),) * 4,
         scratch_shapes=[
             pltpu.SemaphoreType.DMA((ring,)),
             pltpu.SemaphoreType.DMA((ring,)),
@@ -210,7 +203,7 @@
             collective_id=0, has_side_effects=True, vmem_limit_bytes=40 * 1024 * 1024
         ),
         name="scatter_heads",
-    )(q_send, kv_send, weights)
+    )(q_send, kv_send, weights, targets, g_cross[None, :], w_cross)
 
 
 def norm_rows(values, gain):
@@ -551,10 +544,53 @@
     )(mixed, stats, weights, mine, live)
 
 
-def attend_kernel(lengths, q_ref, kv_ref, o_ref, keys, values, count):
+def project_kernel(share, tokens, gain, w_ref, q_out, kv_out):
+    rows = tokens.shape[0]
+    part = rows // share
+    heads = w_ref.shape[2] // HD
+    normed = norm_rows(tokens[...].astype(jnp.float32), gain[...]).astype(jnp.bfloat16)
+    scaling = jnp.bfloat16(HD ** (-0.5))
+    queries = (
+        lax.dot_general(
+            w_ref[0], normed, (((0,), (1,)), ((), ())), preferred_element_type=jnp.float32
+        ).astype(jnp.bfloat16)
+        * scaling
+    )
+    keys = jnp.dot(normed, w_ref[1], preferred_element_type=jnp.float32).astype(jnp.bfloat16)
+    values = jnp.dot(normed, w_ref[2], preferred_element_type=jnp.float32).astype(jnp.bfloat16)
+    for h in range(heads):
+        cut = slice(h * HD, (h + 1) * HD)
+        both = jnp.concatenate([keys[:, cut], values[:, cut]], axis=1)
+        for s in range(share):
+            at = slice(s * part, (s + 1) * part)
+            q_out[h * share + s] = queries[cut, at]
+            kv_out[h * share + s] = both[at, :]
+
+
+def project_heads(share, tokens, gain, weights):
+    rows = tokens.shape[0]
+    heads = weights.shape[2] // HD
+    part = rows // share
+    vmem = pl.BlockSpec(memory_space=pltpu.VMEM)
+    return pl.pallas_call(
+        functools.partial(project_kernel, share),
+        out_shape=(
+            jax.ShapeDtypeStruct((heads * share, HD, part), jnp.bfloat16),
+            jax.ShapeDtypeStruct((heads * share, part, 2 * HD), jnp.bfloat16),
+        ),
+        in_specs=[vmem, vmem, vmem],
+        out_specs=(vmem, vmem),
+        compiler_params=pltpu.CompilerParams(vmem_limit_bytes=40 * 1024 * 1024),
+        name="project_heads",
+    )(tokens, gain[None, :], weights)
+
+
+def attend_kernel(lengths, q_ref, kv_ref, o_ref, keys, values, flipped, count):
     blocks, span, lanes = kv_ref.shape
     tile = span
     queries = q_ref.shape[1]
+    group = math.gcd(queries, 256)
+    ones_rows = flipped.shape[1] - HD
     lane = lax.broadcasted_iota(jnp.int32, (span, lanes), 1)
     row = lax.broadcasted_iota(jnp.int32, (span, lanes), 0)
 
@@ -574,39 +610,49 @@
         values[at, :] = jnp.zeros((span, lanes), jnp.bfloat16)
         count[0] = (stop + tile - 1) // tile
 
+        def flip(t, carry):
+            at = pl.ds(pl.multiple_of(t * tile, tile), tile)
+            flipped[t] = values[at, :].T[HD - ones_rows :, :]
+            return carry
+
+        lax.fori_loop(0, count[0], flip, 0)
+
     spare = lax.broadcasted_iota(jnp.int32, (HD, queries), 0)
     pick = jnp.where(spare == 0, 1.0, 0.0).astype(jnp.bfloat16)
     q_wide = jnp.concatenate([q_ref[...], pick], axis=0)
+    cuts = [slice(g, g + group) for g in range(0, queries, group)]
 
     def step(t, state):
-        top, mixed = state
         at = pl.ds(pl.multiple_of(t * tile, tile), tile)
-        scores = lax.dot_general(
-            keys[at, :], q_wide, (((1,), (0,)), ((), ())), preferred_element_type=jnp.float32
-        )
-        new_top = jnp.maximum(top, jnp.max(scores, axis=0, keepdims=True))
-        weights = jnp.exp(scores - new_top).astype(jnp.bfloat16)
-        part = lax.dot_general(
-            values[at, :], weights, (((0,), (0,)), ((), ())), preferred_element_type=jnp.float32
-        )
-        return new_top, mixed * jnp.exp(top - new_top) + part
-
-    top, mixed = lax.fori_loop(
-        0,
-        count[0],
-        step,
+        keys_here = keys[at, :]
+        values_here = flipped[t]
+        all_scores = [
+            jnp.dot(keys_here, q_wide[:, cut], preferred_element_type=jnp.float32) for cut in cuts
+        ]
+        updated = []
+        for scores, (top, mixed) in zip(all_scores, state):
+            new_top = jnp.maximum(top, jnp.max(scores, axis=0, keepdims=True))
+            weights = jnp.exp(scores - new_top).astype(jnp.bfloat16)
+            part = jnp.dot(values_here, weights, preferred_element_type=jnp.float32)
+            updated.append((new_top, mixed * jnp.exp(top - new_top) + part))
+        return tuple(updated)
+
+    start = tuple(
         (
-            jnp.full((1, queries), masked_score, jnp.float32),
-            jnp.zeros((lanes, queries), jnp.float32),
-        ),
-    )
-    o_ref[...] = (mixed[HD:, :] / mixed[0:1, :]).astype(jnp.bfloat16)
+            jnp.full((1, group), masked_score, jnp.float32),
+            jnp.zeros((ones_rows + HD, group), jnp.float32),
+        )
+        for cut in cuts
+    )
+    ends = lax.fori_loop(0, count[0], step, start)
+    for cut, (top, mixed) in zip(cuts, ends):
+        o_ref[:, cut] = (mixed[ones_rows:, :] / mixed[0:1, :]).astype(jnp.bfloat16)
 
 
 def attend(q_all, kv_all, pad_lengths):
     blocks, span, lanes = kv_all.shape
     total = q_all.shape[1]
-    width = math.gcd(total, 512)
+    width = math.gcd(total, 2048)
     return pl.pallas_call(
         attend_kernel,
         out_shape=jax.ShapeDtypeStruct((HD, total), jnp.bfloat16),
@@ -621,11 +667,12 @@
             scratch_shapes=[
                 pltpu.VMEM(((blocks + 1) * span, lanes), jnp.bfloat16),
                 pltpu.VMEM(((blocks + 1) * span, lanes), jnp.bfloat16),
+                pltpu.VMEM((blocks + 1, HD + 16, span), jnp.bfloat16),
                 pltpu.SMEM((1,), jnp.int32),
             ],
         ),
         compiler_params=pltpu.CompilerParams(
-            dimension_semantics=("arbitrary",), vmem_limit_bytes=40 * 1024 * 1024
+            dimension_semantics=("arbitrary",), vmem_limit_bytes=48 * 1024 * 1024
         ),
         name="attend",
     )(pad_lengths, q_all, kv_all)
@@ -654,29 +701,10 @@
     heads_here = self_qkv.shape[2] // HD
     share = ring // heads_here
     part = row_count // share
-    scaling = HD ** (-0.5)
-    normed = rms_norm(tokens, norm_attn).astype(jnp.bfloat16)
-    q_t = lax.dot_general(
-        self_qkv[0], normed, (((0,), (1,)), ((), ())), preferred_element_type=jnp.float32
-    ).astype(jnp.bfloat16) * jnp.bfloat16(scaling)
-    keys_local = jnp.dot(normed, self_qkv[1], preferred_element_type=jnp.float32).astype(
-        jnp.bfloat16
-    )
-    values_local = jnp.dot(normed, self_qkv[2], preferred_element_type=jnp.float32).astype(
-        jnp.bfloat16
-    )
-    q_send = (
-        q_t.reshape(heads_here, HD, share, part).transpose(0, 2, 1, 3).reshape(ring, HD, part)
-    )
-    kv_local = jnp.concatenate(
-        [
-            keys_local.reshape(row_count, heads_here, HD),
-            values_local.reshape(row_count, heads_here, HD),
-        ],
-        axis=2,
-    )
-    kv_send = kv_local.transpose(1, 0, 2).reshape(ring, part, 2 * HD)
-    q_got, kv_got, out_all = scatter_heads(ring, share, sides, q_send, kv_send, self_out)
+    q_send, kv_send = project_heads(share, tokens, norm_attn, self_qkv)
+    q_got, kv_got, out_all, cross_q = scatter_heads(
+        ring, share, sides, q_send, kv_send, self_out, targets, norm_cross, cross_query
+    )
     q_all = q_got.transpose(1, 0, 2).reshape(HD, ring * part)
     mixed_t = attend(q_all, kv_got, pad_lengths)
     back = mixed_t.reshape(HD, ring, part).transpose(1, 0, 2)
@@ -693,10 +721,6 @@
         ffn_out,
     )
     target_rows = targets.shape[0]
-    cross_normed = rms_norm(targets, norm_cross).astype(jnp.bfloat16)
-    cross_q = jnp.dot(cross_normed, cross_query, preferred_element_type=jnp.float32).astype(
-        jnp.bfloat16
-    ) * jnp.bfloat16(scaling)
     cross_keys = jnp.dot(encoded, cross_kv[0], preferred_element_type=jnp.float32).astype(
         jnp.bfloat16
     )

time: 227 us -> 191 us (0.84)
  Pallas kernels: 192 us -> 172 us
  matrix products: 10.7 us -> 3.01 us
  other arithmetic: 5.34 us -> 0.11 us
  local copies, waits for them, and re-layouts: 15.6 us -> 12.8 us
    pallas_call x1, Pallas kernels: 52.8 us -> 31.1 us  [attend(): pl.pallas_call(attend_kernel, out_shape=jax.ShapeDtypeStruct((HD, total),...]
    dot_general x4 -> x0, matrix products: 9.32 us -> none  [the longest x1 2.78 us: local(): lax.dot_general(self_qkv[0], normed, (((0,), (1,)), ((), ())), preferred_...]
    unnamed x30 -> x44, local copies, waits for them, and re-layouts: 6.28 us -> 12.1 us
    reshape x3 -> x0, local copies, waits for them, and re-layouts: 4.59 us -> none  [the longest x1 1.96 us: local(): q_t.reshape(heads_here, HD, share, part).transpose(0, 2, 1, 3)]
    reduce_sum x2 -> x0, other arithmetic: 3.09 us -> none  [rms_norm(): jnp.mean(widened * widened, axis=-1, keepdims=True) + epsilon]
where the time goes in v3:
time: 191 us; the launch traced here: 189 us
  Pallas kernels  172 us (90%)
  local copies, waits for them, and re-layouts  12.8 us (7%)
  matrix products  3.01 us (2%)
    pallas_call x1, Pallas kernels, encoder_block(): pl.pallas_call(functools.partial(block_kernel, ring, share, sides), out_s...  61.2 us
    pallas_call x1, Pallas kernels, merge_targets(): pl.pallas_call(functools.partial(merge_kernel, ring, sides), out_shape=ja...  38.5 us
    pallas_call x1, Pallas kernels, scatter_heads(): pl.pallas_call(functools.partial(scatter_kernel, ring, share, sides), out...  33.5 us
    pallas_call x1, Pallas kernels, attend(): pl.pallas_call(attend_kernel, out_shape=jax.ShapeDtypeStruct((HD, total),...  31.1 us
    unnamed x44, local copies, waits for them, and re-layouts  12.1 us
    pallas_call x1, Pallas kernels, cross_attend(): pl.pallas_call(cross_kernel, out_shape=(jax.ShapeDtypeStruct((queries, wi...  5.45 us

profile of v3, /device:TPU:0, one launch (start us, length us, event | category | flops | bytes accessed | tf_op | source)
XLA Modules:
  0.0 188.7 jit_solution(13866979218929694918)
XLA Ops:
  0.6 0.0 copy-start
  0.6 1.2 copy-done
  1.9 0.0 copy-start.2
  1.9 1.9 %copy-done.2 = bf16[3,1024,512]{2,1,0:T(8,128)(2,1)S(1)} copy-done((bf16[3,1024,512]{2,1,0:T(8,128)(2,1)S(1)}, bf16[3,1024,512]{2,1,0:T(8,128)(2,1)}, u32[]{:S(2)}) %copy-start.2) | copy-done | bytes 3145752
  3.8 0.0 copy-start.14
  3.8 0.7 copy-done.14
  4.4 0.0 copy-start.4
  4.4 0.0 copy-start.6
  4.4 0.0 copy-start.7
  4.4 0.0 copy-start.17
  4.4 2.2 %project_heads.1 = (bf16[16,64,256]{2,1,0:T(8,128)(2,1)S(1)}, bf16[16,256,128]{2,1,0:T(8,128)(2,1)S(1)}) custom-call(bf16[512,1024]{1,0:T(8,128)(2,1)S(1)} %copy-done, f32[1,1024]{1,0:T(1,128)S(1)} %bitcast.28, bf16[3,1024,512]{2,1,0:T(8,128)(2,1)S(1)} %copy-done.2), custom_call_target="tpu_custom_call" | custom-call | tf_op jit(solution)/shard_map/project_heads/pallas_call | solution.py:575
  6.6 0.0 copy-done.4
  6.6 0.0 copy-done.6
  6.6 0.0 copy-done.7
  6.7 0.0 copy-done.17
  6.7 0.0 copy-start.18
  6.7 33.5 %scatter_heads.1 = (bf16[16,64,256]{2,1,0:T(8,128)(2,1)S(1)}, bf16[16,512,128]{2,1,0:T(8,128)(2,1)S(1)}, bf16[2,512,1024]{2,1,0:T(8,128)(2,1)S(1)}, bf16[512,512]{1,0:T(8,128)(2,1)S(1)}) custom-call(bf16[16,64,256]{2,1,0:T(8,128)(2,1)S(1)} %get-tuple-element.10.q_in, bf16[16,256,128]{2,1,0:T(8,128)(2,1)S(1)} %get-tuple-element.11.kv_in, ...), custom_call_target="tpu_custom_call" | custom-call | tf_op jit(solution)/shard_map/scatter_heads/pallas_call | solution.py:181
  40.2 0.0 copy-start.3
  40.2 1.3 copy-done.3
  41.5 0.0 copy-start.8
  41.5 0.0 copy-done.18
  41.5 0.0 copy-start.1
  41.6 0.0 copy-start.15
  41.6 0.0 copy-start.16
  41.6 31.1 %attend.1 = bf16[64,4096]{1,0:T(8,128)(2,1)S(1)} custom-call(s32[16]{0:T(128)S(1)} %copy-done.18, bf16[64,4096]{1,0:T(8,128)(2,1)S(1)} %bitcast.24, bf16[16,512,128]{2,1,0:T(8,128)(2,1)S(1)} %get-tuple-element.13.kv_ref), custom_call_target="tpu_custom_call" | custom-call | tf_op jit(solution)/shard_map/attend/pallas_call | solution.py:656
  72.7 0.0 copy-done.8
  72.7 0.0 copy-done.1
  72.7 0.0 copy-done.15
  72.7 0.0 copy-done.16
  72.7 0.0 copy-start.19
  72.8 61.2 %encoder_block.1 = bf16[512,1024]{1,0:T(8,128)(2,1)S(1)} custom-call(bf16[16,64,256]{2,1,0:T(8,128)(2,1)S(1)} %bitcast.23, bf16[1024,1024]{1,0:T(8,128)(2,1)} %bitcast.26, bf16[512,1024]{1,0:T(8,128)(2,1)S(1)} %copy-done.1, f32[1,1024]{1,0:T(1,128)S(1)} %bitcast.29, f32[1,1024]{1,0:T(1,128)S(1)} %bitcast.30, bf16[2,1024,1408]{2,1,0:T(8,128)(2,1)} %up_hbm.1, ...), custom_call_target="tpu_custom_call" | custom-call | tf_op jit(solution)/shard_map/encoder_block/pallas_call | solution.py:347
  134.0 0.0 copy-done.19
  134.0 1.5 convolution_convert_fusion.v_ref
  135.5 0.0 copy-start.20
  135.5 0.0 copy-start.5
  135.5 1.5 convolution_convert_fusion.1.k_ref
  137.0 0.6 dynamic_slice.6.length
  137.6 0.0 copy-start.9
  137.6 1.0 copy-done.9
  138.6 0.0 copy-start.10
  138.6 1.0 copy-done.10
  139.7 0.0 copy-start.11
  139.7 1.0 copy-done.11
  140.7 5.4 %cross_attend.1 = (bf16[512,512]{1,0:T(8,128)(2,1)S(1)}, f32[512,128]{1,0:T(8,128)S(1)}) custom-call(s32[1]{0:T(128)} %dynamic_slice.6.length, bf16[512,512]{1,0:T(8,128)(2,1)S(1)} %copy-done.9, bf16[512,512]{1,0:T(8,128)(2,1)S(1)} %copy-done.11, bf16[512,512]{1,0:T(8,128)(2,1)S(1)} %copy-done.10), custom_call_target="tpu_custom_call" | custom-call | tf_op jit(solution)/shard_map/cross_attend/pallas_call | solution.py:788
  146.2 0.0 copy-start.12
  146.2 0.8 copy-done.12
  147.0 0.0 copy-done.20
  147.0 0.1 select_reduce_fusion
  147.1 0.1 broadcast_in_dim.39.live
  147.2 0.0 copy-done.5
  147.2 0.0 copy-start.13
  147.2 1.0 copy-done.13
  148.2 38.5 %merge_targets.1 = bf16[512,1024]{1,0:T(8,128)(2,1)S(1)} custom-call(bf16[512,512]{1,0:T(8,128)(2,1)S(1)} %copy-done.13, f32[512,128]{1,0:T(8,128)S(1)} %get-tuple-element.17.stats, bf16[512,1024]{1,0:T(8,128)(2,1)S(1)} %copy-done.5, bf16[32,1024]{1,0:T(8,128)(2,1)S(1)} %constant_dynamic-slice_fusion.mine, f32[32,1024]{1,0:T(8,128)S(1)} %broadcast_in_dim.39.live), custom_call_target="tpu_custom_call" | custom-call | tf_op jit(solution)/shard_map/merge_targets/pallas_call | solution.py:519
  186.7 1.0 copy.28
  187.7 1.0 copy.29
  (5 shorter events, 0.1 us)
Async XLA Ops:
  0.6 1.2 copy-start
  1.9 1.9 %copy-start.2 = (bf16[3,1024,512]{2,1,0:T(8,128)(2,1)S(1)}, bf16[3,1024,512]{2,1,0:T(8,128)(2,1)}, u32[]{:S(2)}) copy-start(bf16[3,1024,512]{2,1,0:T(8,128)(2,1)} %w_ref.2) | copy-start | bytes 9437188
  3.8 0.7 copy-start.14
  4.4 2.2 %copy-start.4 = (bf16[512,1024]{1,0:T(8,128)(2,1)S(1)}, bf16[512,1024]{1,0:T(8,128)(2,1)}, u32[]{:S(2)}) copy-start(bf16[512,1024]{1,0:T(8,128)(2,1)} %targets.1) | copy-start | bytes 3145732
  4.4 2.2 %copy-start.6 = (bf16[512,1024]{1,0:T(8,128)(2,1)S(1)}, bf16[512,1024]{1,0:T(8,128)(2,1)}, u32[]{:S(2)}) copy-start(bf16[512,1024]{1,0:T(8,128)(2,1)} %w_in.1) | copy-start | bytes 3145732
  4.4 2.2 %copy-start.7 = (bf16[1024,512]{1,0:T(8,128)(2,1)S(1)}, bf16[1024,512]{1,0:T(8,128)(2,1)}, u32[]{:S(2)}) copy-start(bf16[1024,512]{1,0:T(8,128)(2,1)} %w_cross.1) | copy-start | bytes 3145732
  4.4 2.2 %copy-start.17 = (f32[1024]{0:T(1024)S(1)}, f32[1024]{0:T(1024)}, u32[]{:S(2)}) copy-start(f32[1024]{0:T(1024)} %param.26) | copy-start | bytes 12292
  6.7 34.9 %copy-start.18 = (s32[16]{0:T(128)S(1)}, s32[16]{0:T(128)}, u32[]{:S(2)}) copy-start(s32[16]{0:T(128)} %lengths.1) | copy-start | bytes 196
  40.2 1.3 copy-start.3
  41.5 31.2 %copy-start.8 = (bf16[512,512]{1,0:T(8,128)(2,1)}, bf16[512,512]{1,0:T(8,128)(2,1)S(1)}, u32[]{:S(2)}) copy-start(bf16[512,512]{1,0:T(8,128)(2,1)S(1)} %get-tuple-element.15.q_ref) | copy-start | bytes 1572868
  41.5 31.2 %copy-start.1 = (bf16[512,1024]{1,0:T(8,128)(2,1)S(1)}, bf16[512,1024]{1,0:T(8,128)(2,1)}, u32[]{:S(2)}) copy-start(bf16[512,1024]{1,0:T(8,128)(2,1)} %tokens.3) | copy-start | bytes 3145732
  41.6 31.2 %copy-start.15 = (f32[1024]{0:T(1024)S(1)}, f32[1024]{0:T(1024)}, u32[]{:S(2)}) copy-start(f32[1024]{0:T(1024)} %param.19) | copy-start | bytes 12292
  41.6 31.2 %copy-start.16 = (f32[1024]{0:T(1024)S(1)}, f32[1024]{0:T(1024)}, u32[]{:S(2)}) copy-start(f32[1024]{0:T(1024)} %param.22) | copy-start | bytes 12292
  72.7 61.2 %copy-start.19 = (bf16[2,1024,512]{2,1,0:T(8,128)(2,1)S(1)}, bf16[2,1024,512]{2,1,0:T(8,128)(2,1)}, u32[]{:S(2)}) copy-start(bf16[2,1024,512]{2,1,0:T(8,128)(2,1)} %param.28) | copy-start | bytes 6291460
  135.5 11.5 %copy-start.20 = (s32[4]{0:T(128)S(1)}, s32[4]{0:T(128)}, u32[]{:S(2)}) copy-start(s32[4]{0:T(128)} %param.25) | copy-start | bytes 52
  135.5 11.7 %copy-start.5 = (bf16[512,1024]{1,0:T(8,128)(2,1)S(1)}, bf16[512,1024]{1,0:T(8,128)(2,1)}, u32[]{:S(2)}) copy-start(bf16[512,1024]{1,0:T(8,128)(2,1)} %w_ref.3) | copy-start | bytes 3145732
  137.6 1.0 copy-start.9
  138.6 1.0 copy-start.10
  139.7 1.0 copy-start.11
  146.2 0.8 copy-start.12
  147.2 1.0 copy-start.13

commit v4 on v3

--- a/solution.py
+++ b/solution.py
@@ -213,8 +213,10 @@
 
 def block_kernel(
     ring, share, sides, x_in, w_out, tokens, g_ffn, g_final, up_hbm, down_hbm,
-    encoded,
-    context, hidden, normed, parts, up, down, ss, rs, fs, fr, ps, pr, ls,
+    kv_hbm, cross_q, bias,
+    encoded, mixed, stats,
+    context, hidden, normed, parts, up, down, w_kv, cross_k, cross_v,
+    ss, rs, fs, fr, ps, pr, ls,
 ):
     me = lax.axis_index("seq")
     here = lax.axis_index("head")
@@ -222,8 +224,10 @@
     rows, width = tokens.shape
     up_load = pltpu.make_async_copy(up_hbm, up, ls.at[0])
     down_load = pltpu.make_async_copy(down_hbm, down, ls.at[1])
+    kv_load = pltpu.make_async_copy(kv_hbm, w_kv, ls.at[3])
     up_load.start()
     down_load.start()
+    kv_load.start()
 
     def place(side, origin):
         return context.at[lax.rem(origin, share), side * heads + lax.div(origin, share)]
@@ -325,6 +329,7 @@
         return carry
 
     lax.fori_loop(0, chunks, feed, 0)
+    kv_load.wait()
 
     def close(c, carry):
         for k in range(1, sides):
@@ -333,22 +338,68 @@
         total = hidden[span(c), :]
         for side in range(sides):
             total = total + parts[side, span(c), :].astype(jnp.float32)
-        encoded[span(c), :] = norm_rows(total, g_final[...]).astype(jnp.bfloat16)
+        done = norm_rows(total, g_final[...]).astype(jnp.bfloat16)
+        encoded[span(c), :] = done
+        cross_k[span(c), :] = jnp.dot(
+            done, w_kv[0], preferred_element_type=jnp.float32
+        ).astype(jnp.bfloat16)
+        cross_v[span(c), :] = jnp.dot(
+            done, w_kv[1], preferred_element_type=jnp.float32
+        ).astype(jnp.bfloat16)
         return carry
 
     lax.fori_loop(0, chunks, close, 0)
-
-
-def encoder_block(ring, share, sides, back, w_out, tokens, g_ffn, g_final, ffn_in, ffn_out):
+    targets = cross_q.shape[0]
+    lane = lax.broadcasted_iota(jnp.int32, (rows, 2 * HD), 1)
+    out_lane = lax.broadcasted_iota(jnp.int32, (targets, 2 * HD), 1)
+    ones = jnp.ones((rows, 2 * HD), jnp.bfloat16)
+    stats[...] = jnp.where(out_lane < HD, 0.0, 1.0)
+
+    def cross_pair(i, carry):
+        cut = pl.ds(pl.multiple_of(i * 2 * HD, 2 * HD), 2 * HD)
+        q_here = cross_q[:, cut]
+        k_here = cross_k[:, cut]
+        v_here = cross_v[:, cut]
+        pieces = []
+        seen = stats[...]
+        for h in range(2):
+            own = lane < HD if h == 0 else lane >= HD
+            keys = jnp.where(own, k_here, jnp.zeros_like(ones))
+            values = jnp.where(own, v_here, ones)
+            scores = bias[...] + lax.dot_general(
+                q_here, keys, (((1,), (1,)), ((), ())), preferred_element_type=jnp.float32
+            )
+            top = jnp.max(scores, axis=1, keepdims=True)
+            weights = jnp.exp(scores - top).astype(jnp.bfloat16)
+            piece = jnp.dot(weights, values, preferred_element_type=jnp.float32)
+            total = piece[:, 2 * HD - 1 :] if h == 0 else piece[:, :1]
+            seen = jnp.where(
+                out_lane == 2 * i + h, top, jnp.where(out_lane == HD + 2 * i + h, total, seen)
+            )
+            pieces.append(piece)
+        stats[...] = seen
+        mixed[:, cut] = jnp.where(out_lane < HD, pieces[0], pieces[1]).astype(jnp.bfloat16)
+        return carry
+
+    lax.fori_loop(0, heads // 2, cross_pair, 0)
+
+
+def encoder_block(
+    ring, share, sides, back, w_out, tokens, g_ffn, g_final, ffn_in, ffn_out, w_kv, cross_q, bias
+):
     rows, width = tokens.shape
     chunks = rows // math.gcd(rows, 128)
     vmem = pl.BlockSpec(memory_space=pltpu.VMEM)
     hbm = pl.BlockSpec(memory_space=pl.ANY)
     return pl.pallas_call(
         functools.partial(block_kernel, ring, share, sides),
-        out_shape=jax.ShapeDtypeStruct((rows, width), jnp.bfloat16),
-        in_specs=[vmem, vmem, vmem, vmem, vmem, hbm, hbm],
-        out_specs=vmem,
+        out_shape=(
+            jax.ShapeDtypeStruct((rows, width), jnp.bfloat16),
+            jax.ShapeDtypeStruct(cross_q.shape, jnp.bfloat16),
+            jax.ShapeDtypeStruct((cross_q.shape[0], 2 * HD), jnp.float32),
+        ),
+        in_specs=[vmem, vmem, vmem, vmem, vmem, hbm, hbm, hbm, vmem, vmem],
+        out_specs=(vmem, vmem, vmem),
         scratch_shapes=[
             pltpu.VMEM((share, sides * (ring // share), HD, rows // share), jnp.bfloat16),
             pltpu.VMEM((rows, width), jnp.float32),
@@ -356,19 +407,24 @@
             pltpu.VMEM((sides, rows, width), jnp.bfloat16),
             pltpu.VMEM(ffn_in.shape, jnp.bfloat16),
             pltpu.VMEM(ffn_out.shape, jnp.bfloat16),
+            pltpu.VMEM(w_kv.shape, jnp.bfloat16),
+            pltpu.VMEM((rows, w_kv.shape[2]), jnp.bfloat16),
+            pltpu.VMEM((rows, w_kv.shape[2]), jnp.bfloat16),
             pltpu.SemaphoreType.DMA((ring,)),
             pltpu.SemaphoreType.DMA((ring,)),
             pltpu.SemaphoreType.DMA((ring, sides)),
             pltpu.SemaphoreType.DMA((ring, sides)),
             pltpu.SemaphoreType.DMA((chunks, sides)),
             pltpu.SemaphoreType.DMA((chunks, sides)),
-            pltpu.SemaphoreType.DMA((3,)),
+            pltpu.SemaphoreType.DMA((4,)),
         ],
         compiler_params=pltpu.CompilerParams(
             collective_id=1, has_side_effects=True, vmem_limit_bytes=50 * 1024 * 1024
         ),
         name="encoder_block",
-    )(back, w_out, tokens, g_ffn[None, :], g_final[None, :], ffn_in, ffn_out)
+    )(
+        back, w_out, tokens, g_ffn[None, :], g_final[None, :], ffn_in, ffn_out, w_kv, cross_q, bias
+    )
 
 
 def merge_kernel(
@@ -708,7 +764,11 @@
     q_all = q_got.transpose(1, 0, 2).reshape(HD, ring * part)
     mixed_t = attend(q_all, kv_got, pad_lengths)
     back = mixed_t.reshape(HD, ring, part).transpose(1, 0, 2)
-    encoded = encoder_block(
+    my_length = lax.dynamic_slice_in_dim(pad_lengths, lax.axis_index("seq"), 1, 0)
+    bias = jnp.where(
+        jnp.arange(row_count, dtype=jnp.int32)[None, :] < my_length[0], 0.0, masked_score
+    ).astype(jnp.float32)
+    encoded, mixed, stats = encoder_block(
         ring,
         share,
         sides,
@@ -719,16 +779,11 @@
         norm_final,
         ffn_in,
         ffn_out,
+        cross_kv,
+        cross_q,
+        bias,
     )
     target_rows = targets.shape[0]
-    cross_keys = jnp.dot(encoded, cross_kv[0], preferred_element_type=jnp.float32).astype(
-        jnp.bfloat16
-    )
-    cross_values = jnp.dot(encoded, cross_kv[1], preferred_element_type=jnp.float32).astype(
-        jnp.bfloat16
-    )
-    my_length = lax.dynamic_slice_in_dim(pad_lengths, lax.axis_index("seq"), 1, 0)
-    mixed, stats = cross_attend(my_length, cross_q, cross_keys, cross_values)
     slice_rows = target_rows // ring
     slots = lax.axis_index("seq") * slice_rows + jnp.arange(slice_rows, dtype=jnp.int32)
     owner = slots // TGT_LEN
@@ -745,70 +800,6 @@
     live = jnp.broadcast_to(target_live[:, None], mine.shape).astype(jnp.float32)
     decoded = merge_targets(ring, sides, mixed, stats, cross_out, mine, live)
     return (encoded, decoded)
-
-
-def cross_kernel(length, q_ref, k_ref, v_ref, o_ref, stats):
-    i = pl.program_id(0)
-    rows = k_ref.shape[0]
-    queries = q_ref.shape[0]
-    live = lax.broadcasted_iota(jnp.int32, (queries, rows), 1) < length[0]
-    lane = lax.broadcasted_iota(jnp.int32, (rows, 2 * HD), 1)
-    out_lane = lax.broadcasted_iota(jnp.int32, (queries, 2 * HD), 1)
-    ones = jnp.ones((rows, 2 * HD), jnp.bfloat16)
-
-    @pl.when(i == 0)
-    def clear():
-        stats[...] = jnp.where(out_lane < HD, 0.0, 1.0)
-
-    pieces = []
-    for h in range(2):
-        own = lane < HD if h == 0 else lane >= HD
-        keys = jnp.where(own, k_ref[...], jnp.zeros_like(ones))
-        values = jnp.where(own, v_ref[...], ones)
-        scores = lax.dot_general(
-            q_ref[...], keys, (((1,), (1,)), ((), ())), preferred_element_type=jnp.float32
-        )
-        scores = jnp.where(live, scores, masked_score)
-        top = jnp.max(scores, axis=1, keepdims=True)
-        weights = jnp.exp(scores - top).astype(jnp.bfloat16)
-        part = jnp.dot(weights, values, preferred_element_type=jnp.float32)
-        total = part[:, 2 * HD - 1 :] if h == 0 else part[:, :1]
-        stats[...] = jnp.where(
-            out_lane == 2 * i + h,
-            top,
-            jnp.where(out_lane == HD + 2 * i + h, total, stats[...]),
-        )
-        pieces.append(part)
-    o_ref[...] = jnp.where(out_lane < HD, pieces[0], pieces[1]).astype(jnp.bfloat16)
-
-
-def cross_attend(my_length, q_all, keys, values):
-    rows, width = keys.shape
-    queries = q_all.shape[0]
-    return pl.pallas_call(
-        cross_kernel,
-        out_shape=(
-            jax.ShapeDtypeStruct((queries, width), jnp.bfloat16),
-            jax.ShapeDtypeStruct((queries, 2 * HD), jnp.float32),
-        ),
-        grid_spec=pltpu.PrefetchScalarGridSpec(
-            num_scalar_prefetch=1,
-            grid=(width // (2 * HD),),
-            in_specs=[
-                pl.BlockSpec((queries, 2 * HD), lambda i, n: (0, i)),
-                pl.BlockSpec((rows, 2 * HD), lambda i, n: (0, i)),
-                pl.BlockSpec((rows, 2 * HD), lambda i, n: (0, i)),
-            ],
-            out_specs=(
-                pl.BlockSpec((queries, 2 * HD), lambda i, n: (0, i)),
-                pl.BlockSpec((queries, 2 * HD), lambda i, n: (0, 0)),
-            ),
-        ),
-        compiler_params=pltpu.CompilerParams(
-            dimension_semantics=("arbitrary",), vmem_limit_bytes=32 * 1024 * 1024
-        ),
-        name="cross_attend",
-    )(my_length, q_all, keys, values)
 
 
 def solution(mesh):

time: 191 us -> 189 us (0.990)
  matrix products: 3.01 us -> 0 us
  Pallas kernels: 172 us -> 175 us
    pallas_call x1 -> x0, Pallas kernels: 5.45 us -> none  [cross_attend(): pl.pallas_call(cross_kernel, out_shape=(jax.ShapeDtypeStruct((queries, wi...]
    pallas_call x1, Pallas kernels: 61.2 us -> 66.1 us  [encoder_block(): pl.pallas_call(functools.partial(block_kernel, ring, share, sides), out_s...]
    pallas_call x1, Pallas kernels: 31.1 us -> 34.3 us  [attend(): pl.pallas_call(attend_kernel, out_shape=jax.ShapeDtypeStruct((HD, total),...]
    dot_general x2 -> x0, matrix products: 3.01 us -> none  [the longest x1 1.51 us: local(): jnp.dot(encoded, cross_kv[1], preferred_element_type=jnp.float32)]
    unnamed x44 -> x38, local copies, waits for them, and re-layouts: 12.1 us -> 11.1 us
where the time goes in v4:
time: 189 us; the launch traced here: 188 us
  Pallas kernels  175 us (93%)
  local copies, waits for them, and re-layouts  11.9 us (6%)
    pallas_call x1, Pallas kernels, encoder_block(): pl.pallas_call(functools.partial(block_kernel, ring, share, sides), out_s...  66.1 us
    pallas_call x1, Pallas kernels, merge_targets(): pl.pallas_call(functools.partial(merge_kernel, ring, sides), out_shape=ja...  38.5 us
    pallas_call x1, Pallas kernels, attend(): pl.pallas_call(attend_kernel, out_shape=jax.ShapeDtypeStruct((HD, total),...  34.3 us
    pallas_call x1, Pallas kernels, scatter_heads(): pl.pallas_call(functools.partial(scatter_kernel, ring, share, sides), out...  33.5 us
    unnamed x38, local copies, waits for them, and re-layouts  11.1 us

profile of v4, /device:TPU:0, one launch (start us, length us, event | category | flops | bytes accessed | tf_op | source)
XLA Modules:
  0.0 188.0 jit_solution(10551692567357120840)
XLA Ops:
  0.6 0.0 copy-start
  0.6 1.2 copy-done
  1.9 0.0 copy-start.2
  1.9 1.9 %copy-done.2 = bf16[3,1024,512]{2,1,0:T(8,128)(2,1)S(1)} copy-done((bf16[3,1024,512]{2,1,0:T(8,128)(2,1)S(1)}, bf16[3,1024,512]{2,1,0:T(8,128)(2,1)}, u32[]{:S(2)}) %copy-start.2) | copy-done | bytes 3145752
  3.8 0.0 copy-start.12
  3.8 0.7 copy-done.12
  4.4 0.0 copy-start.4
  4.4 0.0 copy-start.8
  4.4 0.0 copy-start.9
  4.4 0.0 copy-start.15
  4.4 2.2 %project_heads.1 = (bf16[16,64,256]{2,1,0:T(8,128)(2,1)S(1)}, bf16[16,256,128]{2,1,0:T(8,128)(2,1)S(1)}) custom-call(bf16[512,1024]{1,0:T(8,128)(2,1)S(1)} %copy-done, f32[1,1024]{1,0:T(1,128)S(1)} %bitcast.21, bf16[3,1024,512]{2,1,0:T(8,128)(2,1)S(1)} %copy-done.2), custom_call_target="tpu_custom_call" | custom-call | tf_op jit(solution)/shard_map/project_heads/pallas_call | solution.py:631
  6.6 0.0 copy-done.4
  6.6 0.0 copy-done.8
  6.6 0.0 copy-done.9
  6.7 0.0 copy-done.15
  6.7 0.0 copy-start.16
  6.7 33.5 %scatter_heads.1 = (bf16[16,64,256]{2,1,0:T(8,128)(2,1)S(1)}, bf16[16,512,128]{2,1,0:T(8,128)(2,1)S(1)}, bf16[2,512,1024]{2,1,0:T(8,128)(2,1)S(1)}, bf16[512,512]{1,0:T(8,128)(2,1)S(1)}) custom-call(bf16[16,64,256]{2,1,0:T(8,128)(2,1)S(1)} %get-tuple-element.11.q_in, bf16[16,256,128]{2,1,0:T(8,128)(2,1)S(1)} %get-tuple-element.12.kv_in, ...), custom_call_target="tpu_custom_call" | custom-call | tf_op jit(solution)/shard_map/scatter_heads/pallas_call | solution.py:181
  40.2 0.0 copy-start.3
  40.2 1.3 copy-done.3
  41.5 0.0 copy-start.1
  41.5 0.0 copy-start.13
  41.5 0.0 copy-start.14
  41.5 0.0 copy-done.16
  41.6 34.3 %attend.1 = bf16[64,4096]{1,0:T(8,128)(2,1)S(1)} custom-call(s32[16]{0:T(128)S(1)} %copy-done.16, bf16[64,4096]{1,0:T(8,128)(2,1)S(1)} %bitcast.18, bf16[16,512,128]{2,1,0:T(8,128)(2,1)S(1)} %get-tuple-element.14.kv_ref), custom_call_target="tpu_custom_call" | custom-call | tf_op jit(solution)/shard_map/attend/pallas_call | solution.py:712
  75.9 0.6 dynamic_slice.6
  76.5 0.6 compare_select_fusion.bias
  77.1 0.0 copy-done.1
  77.1 0.0 copy-done.13
  77.2 0.0 copy-done.14
  77.2 0.0 copy-start.17
  77.2 66.1 %encoder_block.1 = (bf16[512,1024]{1,0:T(8,128)(2,1)S(1)}, bf16[512,512]{1,0:T(8,128)(2,1)S(1)}, f32[512,128]{1,0:T(8,128)S(1)}) custom-call(bf16[16,64,256]{2,1,0:T(8,128)(2,1)S(1)} %bitcast.17, bf16[1024,1024]{1,0:T(8,128)(2,1)} %bitcast.16, bf16[512,1024]{1,0:T(8,128)(2,1)S(1)} %copy-done.1, f32[1,1024]{1,0:T(1,128)S(1)} %bitcast.22, ...), custom_call_target="tpu_custom_call" | custom-call | tf_op jit(solution)/shard_map/encoder_block/pallas_call | solution.py:394
  143.2 0.0 copy-start.6
  143.3 1.0 copy-done.6
  144.2 0.0 copy-start.10
  144.2 0.8 copy-done.10
  145.0 0.0 copy-done.17
  145.0 0.1 select_reduce_fusion
  145.1 0.1 broadcast_in_dim.50.live
  145.2 0.0 copy-start.5
  145.2 1.2 copy-done.5
  146.4 0.0 copy-start.11
  146.4 1.0 copy-done.11
  147.5 0.0 copy-start.7
  147.5 38.5 %merge_targets.1 = bf16[512,1024]{1,0:T(8,128)(2,1)S(1)} custom-call(bf16[512,512]{1,0:T(8,128)(2,1)S(1)} %copy-done.11, f32[512,128]{1,0:T(8,128)S(1)} %get-tuple-element.19.stats, bf16[512,1024]{1,0:T(8,128)(2,1)S(1)} %copy-done.5, bf16[32,1024]{1,0:T(8,128)(2,1)S(1)} %constant_dynamic-slice_fusion.mine, f32[32,1024]{1,0:T(8,128)S(1)} %broadcast_in_dim.50.live), custom_call_target="tpu_custom_call" | custom-call | tf_op jit(solution)/shard_map/merge_targets/pallas_call | solution.py:575
  186.0 0.0 copy-done.7
  186.0 1.0 copy.28
  187.0 1.0 copy.29
  (5 shorter events, 0.1 us)
Async XLA Ops:
  0.6 1.2 copy-start
  1.9 1.9 %copy-start.2 = (bf16[3,1024,512]{2,1,0:T(8,128)(2,1)S(1)}, bf16[3,1024,512]{2,1,0:T(8,128)(2,1)}, u32[]{:S(2)}) copy-start(bf16[3,1024,512]{2,1,0:T(8,128)(2,1)} %w_ref.2) | copy-start | bytes 9437188
  3.8 0.7 copy-start.12
  4.4 2.2 %copy-start.4 = (bf16[512,1024]{1,0:T(8,128)(2,1)S(1)}, bf16[512,1024]{1,0:T(8,128)(2,1)}, u32[]{:S(2)}) copy-start(bf16[512,1024]{1,0:T(8,128)(2,1)} %targets.1) | copy-start | bytes 3145732
  4.4 2.2 %copy-start.8 = (bf16[512,1024]{1,0:T(8,128)(2,1)S(1)}, bf16[512,1024]{1,0:T(8,128)(2,1)}, u32[]{:S(2)}) copy-start(bf16[512,1024]{1,0:T(8,128)(2,1)} %w_in.1) | copy-start | bytes 3145732
  4.4 2.2 %copy-start.9 = (bf16[1024,512]{1,0:T(8,128)(2,1)S(1)}, bf16[1024,512]{1,0:T(8,128)(2,1)}, u32[]{:S(2)}) copy-start(bf16[1024,512]{1,0:T(8,128)(2,1)} %w_cross.1) | copy-start | bytes 3145732
  4.4 2.2 %copy-start.15 = (f32[1024]{0:T(1024)S(1)}, f32[1024]{0:T(1024)}, u32[]{:S(2)}) copy-start(f32[1024]{0:T(1024)} %param.26) | copy-start | bytes 12292
  6.7 34.9 %copy-start.16 = (s32[16]{0:T(128)S(1)}, s32[16]{0:T(128)}, u32[]{:S(2)}) copy-start(s32[16]{0:T(128)} %lengths.1) | copy-start | bytes 196
  40.2 1.3 copy-start.3
  41.5 35.6 %copy-start.1 = (bf16[512,1024]{1,0:T(8,128)(2,1)S(1)}, bf16[512,1024]{1,0:T(8,128)(2,1)}, u32[]{:S(2)}) copy-start(bf16[512,1024]{1,0:T(8,128)(2,1)} %tokens.3) | copy-start | bytes 3145732
  41.5 35.6 %copy-start.13 = (f32[1024]{0:T(1024)S(1)}, f32[1024]{0:T(1024)}, u32[]{:S(2)}) copy-start(f32[1024]{0:T(1024)} %param.19) | copy-start | bytes 12292
  41.5 35.7 %copy-start.14 = (f32[1024]{0:T(1024)S(1)}, f32[1024]{0:T(1024)}, u32[]{:S(2)}) copy-start(f32[1024]{0:T(1024)} %param.22) | copy-start | bytes 12292
  77.2 67.9 %copy-start.17 = (s32[4]{0:T(128)S(1)}, s32[4]{0:T(128)}, u32[]{:S(2)}) copy-start(s32[4]{0:T(128)} %param.25) | copy-start | bytes 52
  143.2 1.0 copy-start.6
  144.2 0.8 copy-start.10
  145.2 1.2 copy-start.5
  146.4 1.0 copy-start.11
  147.5 38.5 %copy-start.7 = (bf16[512,1024]{1,0:T(8,128)(2,1)S(1)}, bf16[512,1024]{1,0:T(8,128)(2,1)}, u32[]{:S(2)}) copy-start(bf16[512,1024]{1,0:T(8,128)(2,1)} %copy-done.6) | copy-start | bytes 3145732

commit v5 on v4

--- a/solution.py
+++ b/solution.py
@@ -213,10 +213,10 @@
 
 def block_kernel(
     ring, share, sides, x_in, w_out, tokens, g_ffn, g_final, up_hbm, down_hbm,
-    kv_hbm, cross_q, bias,
-    encoded, mixed, stats,
+    kv_hbm, cross_q, bias, w_cross, mine, live,
+    encoded, decoded,
     context, hidden, normed, parts, up, down, w_kv, cross_k, cross_v,
-    ss, rs, fs, fr, ps, pr, ls,
+    mixed, stats, ss, rs, fs, fr, ps, pr, ls, *tail
 ):
     me = lax.axis_index("seq")
     here = lax.axis_index("head")
@@ -382,10 +382,12 @@
         return carry
 
     lax.fori_loop(0, heads // 2, cross_pair, 0)
+    merge_tail(ring, sides, mixed, stats, w_cross, mine, live, decoded, *tail)
 
 
 def encoder_block(
-    ring, share, sides, back, w_out, tokens, g_ffn, g_final, ffn_in, ffn_out, w_kv, cross_q, bias
+    ring, share, sides, back, w_out, tokens, g_ffn, g_final, ffn_in, ffn_out, w_kv, cross_q, bias,
+    w_cross, mine, live,
 ):
     rows, width = tokens.shape
     chunks = rows // math.gcd(rows, 128)
@@ -395,11 +397,10 @@
         functools.partial(block_kernel, ring, share, sides),
         out_shape=(
             jax.ShapeDtypeStruct((rows, width), jnp.bfloat16),
-            jax.ShapeDtypeStruct(cross_q.shape, jnp.bfloat16),
-            jax.ShapeDtypeStruct((cross_q.shape[0], 2 * HD), jnp.float32),
+            jax.ShapeDtypeStruct((cross_q.shape[0], width), jnp.bfloat16),
         ),
-        in_specs=[vmem, vmem, vmem, vmem, vmem, hbm, hbm, hbm, vmem, vmem],
-        out_specs=(vmem, vmem, vmem),
+        in_specs=[vmem] * 5 + [hbm] * 3 + [vmem] * 5,
+        out_specs=(vmem, vmem),
         scratch_shapes=[
             pltpu.VMEM((share, sides * (ring // share), HD, rows // share), jnp.bfloat16),
             pltpu.VMEM((rows, width), jnp.float32),
@@ -410,6 +411,8 @@
             pltpu.VMEM(w_kv.shape, jnp.bfloat16),
             pltpu.VMEM((rows, w_kv.shape[2]), jnp.bfloat16),
             pltpu.VMEM((rows, w_kv.shape[2]), jnp.bfloat16),
+            pltpu.VMEM(cross_q.shape, jnp.bfloat16),
+            pltpu.VMEM((cross_q.shape[0], 2 * HD), jnp.float32),
             pltpu.SemaphoreType.DMA((ring,)),
             pltpu.SemaphoreType.DMA((ring,)),
             pltpu.SemaphoreType.DMA((ring, sides)),
@@ -417,17 +420,32 @@
             pltpu.SemaphoreType.DMA((chunks, sides)),
             pltpu.SemaphoreType.DMA((chunks, sides)),
             pltpu.SemaphoreType.DMA((4,)),
+            pltpu.VMEM((ring, mine.shape[0], cross_q.shape[1]), jnp.bfloat16),
+            pltpu.VMEM((ring, mine.shape[0], 2 * HD), jnp.float32),
+            pltpu.VMEM((sides, mine.shape[0], width), jnp.bfloat16),
+            pltpu.SemaphoreType.DMA((ring,)),
+            pltpu.SemaphoreType.DMA((ring,)),
+            pltpu.SemaphoreType.DMA((ring,)),
+            pltpu.SemaphoreType.DMA((ring,)),
+            pltpu.SemaphoreType.DMA((sides,)),
+            pltpu.SemaphoreType.DMA((sides,)),
+            pltpu.SemaphoreType.DMA((ring,)),
+            pltpu.SemaphoreType.DMA((ring,)),
+            pltpu.SemaphoreType.DMA((ring,)),
+            pltpu.SemaphoreType.DMA((ring,)),
+            pltpu.SemaphoreType.DMA((2,)),
         ],
         compiler_params=pltpu.CompilerParams(
             collective_id=1, has_side_effects=True, vmem_limit_bytes=50 * 1024 * 1024
         ),
         name="encoder_block",
     )(
-        back, w_out, tokens, g_ffn[None, :], g_final[None, :], ffn_in, ffn_out, w_kv, cross_q, bias
-    )
-
-
-def merge_kernel(
+        back, w_out, tokens, g_ffn[None, :], g_final[None, :], ffn_in, ffn_out, w_kv, cross_q, bias,
+        w_cross, mine, live,
+    )
+
+
+def merge_tail(
     ring, sides, mixed, stats, w_ref, mine, live, decoded,
     got, got_stats, parts, ms, mr, ts, tr, ps, pr, ds, dr, fs, fr, ls,
 ):
@@ -443,7 +461,6 @@
     own_stats = pltpu.make_async_copy(stats.at[slab(me)], got_stats.at[me], ls.at[1])
     own_mixed.start()
     own_stats.start()
-    greet_all(ring, sides)
 
     def copies(i, origin):
         to = lax.rem(me + i, ring)
@@ -566,38 +583,6 @@
         return carry
 
     lax.fori_loop(0, ring // 2, drain, 0)
-
-
-def merge_targets(ring, sides, mixed, stats, weights, mine, live):
-    rows, width = mine.shape
-    vmem = pl.BlockSpec(memory_space=pltpu.VMEM)
-    dma = pltpu.SemaphoreType.DMA
-    return pl.pallas_call(
-        functools.partial(merge_kernel, ring, sides),
-        out_shape=jax.ShapeDtypeStruct((rows * ring, width), jnp.bfloat16),
-        in_specs=[vmem] * 5,
-        out_specs=vmem,
-        scratch_shapes=[
-            pltpu.VMEM((ring, rows, mixed.shape[1]), jnp.bfloat16),
-            pltpu.VMEM((ring, rows, stats.shape[1]), jnp.float32),
-            pltpu.VMEM((sides, rows, width), jnp.bfloat16),
-            dma((ring,)),
-            dma((ring,)),
-            dma((ring,)),
-            dma((ring,)),
-            dma((sides,)),
-            dma((sides,)),
-            dma((ring,)),
-            dma((ring,)),
-            dma((ring,)),
-            dma((ring,)),
-            dma((2,)),
-        ],
-        compiler_params=pltpu.CompilerParams(
-            collective_id=2, has_side_effects=True, vmem_limit_bytes=40 * 1024 * 1024
-        ),
-        name="merge_targets",
-    )(mixed, stats, weights, mine, live)
 
 
 def project_kernel(share, tokens, gain, w_ref, q_out, kv_out):
@@ -768,7 +753,22 @@
     bias = jnp.where(
         jnp.arange(row_count, dtype=jnp.int32)[None, :] < my_length[0], 0.0, masked_score
     ).astype(jnp.float32)
-    encoded, mixed, stats = encoder_block(
+    target_rows = targets.shape[0]
+    slice_rows = target_rows // ring
+    slots = lax.axis_index("seq") * slice_rows + jnp.arange(slice_rows, dtype=jnp.int32)
+    owner = slots // TGT_LEN
+    limits = jnp.sum(
+        jnp.where(
+            owner[:, None] == jnp.arange(target_lengths.shape[0])[None, :],
+            target_lengths[None, :],
+            0,
+        ),
+        axis=1,
+    )
+    target_live = slots % TGT_LEN < limits
+    mine = lax.dynamic_slice_in_dim(targets, lax.axis_index("seq") * slice_rows, slice_rows, 0)
+    live = jnp.broadcast_to(target_live[:, None], mine.shape).astype(jnp.float32)
+    encoded, decoded = encoder_block(
         ring,
         share,
         sides,
@@ -782,23 +782,10 @@
         cross_kv,
         cross_q,
         bias,
-    )
-    target_rows = targets.shape[0]
-    slice_rows = target_rows // ring
-    slots = lax.axis_index("seq") * slice_rows + jnp.arange(slice_rows, dtype=jnp.int32)
-    owner = slots // TGT_LEN
-    limits = jnp.sum(
-        jnp.where(
-            owner[:, None] == jnp.arange(target_lengths.shape[0])[None, :],
-            target_lengths[None, :],
-            0,
-        ),
-        axis=1,
-    )
-    target_live = slots % TGT_LEN < limits
-    mine = lax.dynamic_slice_in_dim(targets, lax.axis_index("seq") * slice_rows, slice_rows, 0)
-    live = jnp.broadcast_to(target_live[:, None], mine.shape).astype(jnp.float32)
-    decoded = merge_targets(ring, sides, mixed, stats, cross_out, mine, live)
+        cross_out,
+        mine,
+        live,
+    )
     return (encoded, decoded)
 
 

time: 189 us -> 180 us (0.952)
  Pallas kernels: 175 us -> 168 us
  local copies, waits for them, and re-layouts: 11.9 us -> 7.85 us
    pallas_call x1 -> x0, Pallas kernels: 38.5 us -> none  [merge_targets(): pl.pallas_call(functools.partial(merge_kernel, ring, sides), out_shape=ja...]
    pallas_call x1, Pallas kernels: 66.1 us -> 102 us  [encoder_block(): pl.pallas_call(functools.partial(block_kernel, ring, share, sides), out_s...]
    unnamed x38 -> x26, local copies, waits for them, and re-layouts: 11.1 us -> 7.09 us
    pallas_call x1, Pallas kernels: 34.3 us -> 31.1 us  [attend(): pl.pallas_call(attend_kernel, out_shape=jax.ShapeDtypeStruct((HD, total),...]
where the time goes in v5:
time: 180 us; the launch traced here: 178 us
  Pallas kernels  168 us (93%)
  local copies, waits for them, and re-layouts  7.85 us (4%)
    pallas_call x1, Pallas kernels, encoder_block(): pl.pallas_call(functools.partial(block_kernel, ring, share, sides), out_s...  102 us
    pallas_call x1, Pallas kernels, scatter_heads(): pl.pallas_call(functools.partial(scatter_kernel, ring, share, sides), out...  33.5 us
    pallas_call x1, Pallas kernels, attend(): pl.pallas_call(attend_kernel, out_shape=jax.ShapeDtypeStruct((HD, total),...  31.1 us
    unnamed x26, local copies, waits for them, and re-layouts  7.09 us

profile of v5, /device:TPU:0, one launch (start us, length us, event | category | flops | bytes accessed | tf_op | source)
XLA Modules:
  0.0 177.8 jit_solution(7885590651572472929)
XLA Ops:
  0.6 0.0 copy-start
  0.6 1.2 copy-done
  1.9 0.0 copy-start.1
  1.9 1.9 %copy-done.1 = bf16[3,1024,512]{2,1,0:T(8,128)(2,1)S(1)} copy-done((bf16[3,1024,512]{2,1,0:T(8,128)(2,1)S(1)}, bf16[3,1024,512]{2,1,0:T(8,128)(2,1)}, u32[]{:S(2)}) %copy-start.1) | copy-done | bytes 3145752
  3.8 0.0 copy-start.6
  3.8 0.7 copy-done.6
  4.4 0.0 copy-start.3
  4.4 0.0 copy-start.4
  4.4 0.0 copy-start.5
  4.4 0.0 copy-start.7
  4.4 2.2 %project_heads.1 = (bf16[16,64,256]{2,1,0:T(8,128)(2,1)S(1)}, bf16[16,256,128]{2,1,0:T(8,128)(2,1)S(1)}) custom-call(bf16[512,1024]{1,0:T(8,128)(2,1)S(1)} %copy-done, f32[1,1024]{1,0:T(1,128)S(1)} %bitcast.21, bf16[3,1024,512]{2,1,0:T(8,128)(2,1)S(1)} %copy-done.1), custom_call_target="tpu_custom_call" | custom-call | tf_op jit(solution)/shard_map/project_heads/pallas_call | solution.py:616
  6.6 0.0 copy-done.3
  6.6 0.0 copy-done.4
  6.6 0.0 copy-done.5
  6.7 0.0 copy-done.7
  6.7 0.0 copy-start.10
  6.7 33.5 %scatter_heads.1 = (bf16[16,64,256]{2,1,0:T(8,128)(2,1)S(1)}, bf16[16,512,128]{2,1,0:T(8,128)(2,1)S(1)}, bf16[2,512,1024]{2,1,0:T(8,128)(2,1)S(1)}, bf16[512,512]{1,0:T(8,128)(2,1)S(1)}) custom-call(bf16[16,64,256]{2,1,0:T(8,128)(2,1)S(1)} %get-tuple-element.8.q_in, bf16[16,256,128]{2,1,0:T(8,128)(2,1)S(1)} %get-tuple-element.9.kv_in, ...), custom_call_target="tpu_custom_call" | custom-call | tf_op jit(solution)/shard_map/scatter_heads/pallas_call | solution.py:181
  40.2 0.0 copy-start.2
  40.2 1.3 copy-done.2
  41.5 0.0 copy-start.11
  41.5 0.0 copy-start.8
  41.5 0.0 copy-start.9
  41.5 0.0 copy-done.10
  41.5 31.1 %attend.1 = bf16[64,4096]{1,0:T(8,128)(2,1)S(1)} custom-call(s32[16]{0:T(128)S(1)} %copy-done.10, bf16[64,4096]{1,0:T(8,128)(2,1)S(1)} %bitcast.17, bf16[16,512,128]{2,1,0:T(8,128)(2,1)S(1)} %get-tuple-element.11.kv_ref), custom_call_target="tpu_custom_call" | custom-call | tf_op jit(solution)/shard_map/attend/pallas_call | solution.py:697
  72.7 0.6 dynamic_slice.6
  73.3 0.6 compare_select_fusion.bias
  74.0 0.0 copy-done.11
  74.0 0.1 select_reduce_fusion
  74.1 0.1 broadcast_in_dim.50.live
  74.2 0.0 copy-done.8
  74.2 0.0 copy-done.9
  74.2 101.6 %encoder_block.1 = (bf16[512,1024]{1,0:T(8,128)(2,1)S(1)}, bf16[512,1024]{1,0:T(8,128)(2,1)S(1)}) custom-call(bf16[16,64,256]{2,1,0:T(8,128)(2,1)S(1)} %bitcast.16, bf16[1024,1024]{1,0:T(8,128)(2,1)} %bitcast.19, bf16[512,1024]{1,0:T(8,128)(2,1)} %tokens.3, f32[1,1024]{1,0:T(1,128)S(1)} %bitcast.23, f32[1,1024]{1,0:T(1,128)S(1)} %bitcast.24, ...), custom_call_target="tpu_custom_call" | custom-call | tf_op jit(solution)/shard_map/encoder_block/pallas_call | solution.py:396
  175.8 1.0 copy.28
  176.8 1.0 copy.29
  (5 shorter events, 0.1 us)
Async XLA Ops:
  0.6 1.2 copy-start
  1.9 1.9 %copy-start.1 = (bf16[3,1024,512]{2,1,0:T(8,128)(2,1)S(1)}, bf16[3,1024,512]{2,1,0:T(8,128)(2,1)}, u32[]{:S(2)}) copy-start(bf16[3,1024,512]{2,1,0:T(8,128)(2,1)} %w_ref.1) | copy-start | bytes 9437188
  3.8 0.7 copy-start.6
  4.4 2.2 %copy-start.3 = (bf16[512,1024]{1,0:T(8,128)(2,1)S(1)}, bf16[512,1024]{1,0:T(8,128)(2,1)}, u32[]{:S(2)}) copy-start(bf16[512,1024]{1,0:T(8,128)(2,1)} %targets.1) | copy-start | bytes 3145732
  4.4 2.2 %copy-start.4 = (bf16[512,1024]{1,0:T(8,128)(2,1)S(1)}, bf16[512,1024]{1,0:T(8,128)(2,1)}, u32[]{:S(2)}) copy-start(bf16[512,1024]{1,0:T(8,128)(2,1)} %w_in.1) | copy-start | bytes 3145732
  4.4 2.2 %copy-start.5 = (bf16[1024,512]{1,0:T(8,128)(2,1)S(1)}, bf16[1024,512]{1,0:T(8,128)(2,1)}, u32[]{:S(2)}) copy-start(bf16[1024,512]{1,0:T(8,128)(2,1)} %w_cross.2) | copy-start | bytes 3145732
  4.4 2.2 %copy-start.7 = (f32[1024]{0:T(1024)S(1)}, f32[1024]{0:T(1024)}, u32[]{:S(2)}) copy-start(f32[1024]{0:T(1024)} %param.26) | copy-start | bytes 12292
  6.7 34.9 %copy-start.10 = (s32[16]{0:T(128)S(1)}, s32[16]{0:T(128)}, u32[]{:S(2)}) copy-start(s32[16]{0:T(128)} %lengths.1) | copy-start | bytes 196
  40.2 1.3 copy-start.2
  41.5 32.5 %copy-start.11 = (s32[4]{0:T(128)S(1)}, s32[4]{0:T(128)}, u32[]{:S(2)}) copy-start(s32[4]{0:T(128)} %param.25) | copy-start | bytes 52
  41.5 32.7 %copy-start.8 = (f32[1024]{0:T(1024)S(1)}, f32[1024]{0:T(1024)}, u32[]{:S(2)}) copy-start(f32[1024]{0:T(1024)} %param.19) | copy-start | bytes 12292
  41.5 32.7 %copy-start.9 = (f32[1024]{0:T(1024)S(1)}, f32[1024]{0:T(1024)}, u32[]{:S(2)}) copy-start(f32[1024]{0:T(1024)} %param.22) | copy-start | bytes 12292
